TPU v7x, 32 devices: a whole 2x2x4 slice. The times are simulated.
32 devices in a mesh: grid: 8 (over y, x, core), atom: 4 (over z).
Axes of the slice: x: 2, y: 2, z: 4, core: 2. Of those that a mesh axis runs over, the one named last changes fastest.
Arguments:
- basis_values: bfloat16 [64, 128, 512], P(('grid', 'atom')), may hold values from -8 to 8
- block_lists: int32 [64, 4], P('grid'), may hold values from 0 to 95, as said below
- orbitals: bfloat16 [12288, 4096], P('grid', 'atom'), may hold values from -0.00390625 to 0.00390625
- point_weights: float32 [8192], P(('grid', 'atom')), may hold values from 0.1 to 1
- point_atoms: int32 [8192], P(('grid', 'atom')), may hold values from 0 to 127, as said below
- embed_scale: float32 [256], replicated, may hold values from -4 to 4
- embed_shift: float32 [256], replicated, may hold values from -3 to 3
- message_weight: bfloat16 [2, 256, 256], replicated, may hold values from -0.375 to 0.375
- atom_weight: bfloat16 [2, 256, 256], replicated, may hold values from -0.375 to 0.375
- head_weight: float32 [256], replicated, may hold values from -0.375 to 0.375
Outputs:
- fock_orbitals: float32 [12288, 4096], P('grid', 'atom')
- potential: float32 [8192], P(('grid', 'atom'))
Inputs may be any that keep to these rules, and one draw needn't show every extreme that they name: `block_lists`: each row names 4 different blocks; a batch b of group g = b // 8 names only blocks (g - 1) * 12 to (g + 2) * 12 - 1. `point_atoms`: the 256 points of one device name atom centres of one run of max(8, 1) consecutive centres, counted round.
All inputs are finite; a program needn't handle non-finite values.
Results may differ from a plain program's by a relative error of at most 0.04.
Values may be sent and summed in bfloat16 or wider, within the bound.
A program may use at most 128 MiB of HBM per device.

v0:
```python
import functools
import jax
import jax.numpy as jnp
from jax import lax
from jax.experimental import pallas as pl
from jax.experimental.pallas import tpu as pltpu
from jax.sharding import PartitionSpec as P

ATOM_DEV = 32
RUN = max(ATOM_DEV // 4, 1)
LANES = 128
VMEM = pl.BlockSpec(memory_space=pltpu.VMEM)
MESH = pl.DeviceIdType.MESH


def wait_bytes(ref, sem):
    pltpu.make_async_copy(ref, ref, sem).wait()


class Halo:
    def __init__(self, n_grid, rounds, source, low, high, relay, sent, got, passed):
        self.n_grid, self.rounds, self.middle = n_grid, rounds, n_grid // 2
        self.source, self.low, self.high, self.relay = source, low, high, relay
        self.sent, self.got, self.passed = sent, got, passed
        self.size = source.shape[0] // (2 * rounds)
        self.grid, self.atom = lax.axis_index("grid"), lax.axis_index("atom")

    def copy(self, source, target, sent, got, grid):
        pltpu.make_async_remote_copy(
            src_ref=source,
            dst_ref=target,
            send_sem=sent,
            recv_sem=got,
            device_id=(grid, self.atom),
            device_id_type=MESH,
        ).start()

    def send(self, r):
        grid, last, size = self.grid, self.n_grid - 1, self.size
        for way, (step, held, split, able) in enumerate(
            (
                (1, self.low, self.middle - 1, grid < last),
                (-1, self.high, self.middle, grid > 0),
            )
        ):
            for side, end in enumerate((0, last)):
                part = pl.ds((side * self.rounds + r) * size, size)

                @pl.when(jnp.logical_and(able, grid != split))
                def _():
                    self.copy(
                        self.source.at[part], held.at[part],
                        self.sent.at[way], self.got.at[way], grid + step,
                    )

                @pl.when(grid == split)
                def _():
                    self.copy(
                        self.source.at[part], self.relay.at[way, pl.ds(r * size, size)],
                        self.sent.at[way], self.passed.at[way, r], end,
                    )

    def forward(self, r):
        size = self.size
        for side, end in enumerate((0, self.n_grid - 1)):

            @pl.when(self.grid == end)
            def _():
                for way, (held, to) in enumerate(
                    ((self.low, self.middle), (self.high, self.middle - 1))
                ):
                    piece = self.relay.at[way, pl.ds(r * size, size)]
                    wait_bytes(piece, self.passed.at[way, r])
                    part = pl.ds((side * self.rounds + r) * size, size)
                    self.copy(piece, held.at[part], self.sent.at[2 + way], self.got.at[way], to)

    def finish(self):
        grid, last = self.grid, self.n_grid - 1

        @pl.when(grid > 0)
        def _():
            wait_bytes(self.low, self.got.at[0])
            wait_bytes(self.source, self.sent.at[1])

        @pl.when(grid < last)
        def _():
            wait_bytes(self.high, self.got.at[1])
            wait_bytes(self.source, self.sent.at[0])

        @pl.when(jnp.logical_or(grid == 0, grid == last))
        def _():
            for way in range(2):
                wait_bytes(self.relay.at[way], self.sent.at[2 + way])


def halo_scratch(rounds):
    return [
        pltpu.SemaphoreType.DMA((4,)),
        pltpu.SemaphoreType.DMA((2,)),
        pltpu.SemaphoreType.DMA((2, rounds)),
    ]


def meet_all(shape):
    n_grid, n_atom = shape
    n = n_grid * n_atom
    me = lax.axis_index("grid") * n_atom + lax.axis_index("atom")
    barrier = pltpu.get_barrier_semaphore()

    @pl.loop(1, n)
    def _(d):
        t = lax.rem(me + d, n)
        pl.semaphore_signal(
            barrier, inc=1, device_id=(t // n_atom, lax.rem(t, n_atom)), device_id_type=MESH
        )

    pl.semaphore_wait(barrier, n - 1)


ROUNDS = 4


def halo_kernel(
    shape, own, piece, names, low, high, basis, all_names, relay,
    sent, got, passed, piece_sent, piece_got, name_sent, name_got, line_sent, line_got,
):
    n_grid, n_atom = shape
    grid, atom = lax.axis_index("grid"), lax.axis_index("atom")
    meet_all(shape)
    halo = Halo(n_grid, ROUNDS, own, low, high, relay, sent, got, passed)

    def send(source, target, sent_sem, got_sem, to):
        pltpu.make_async_remote_copy(
            src_ref=source,
            dst_ref=target,
            send_sem=sent_sem,
            recv_sem=got_sem,
            device_id=to,
            device_id_type=MESH,
        ).start()

    sides = ((0, 1, grid < n_grid - 1, grid > 0), (2, -1, grid > 0, grid < n_grid - 1))
    for slot, step, able, _ in sides:

        @pl.when(able)
        def _():
            send(names, all_names.at[slot], name_sent.at[slot], name_got.at[slot], (grid + step, atom))
            send(piece, basis.at[slot, atom], piece_sent.at[slot], piece_got.at[slot], (grid + step, atom))

    for r in range(ROUNDS):
        halo.send(r)

    def line(slot, d, way):
        origin = atom - (d - 1) if way == 0 else atom + (d - 1)
        able = (
            jnp.logical_and(atom < n_atom - 1, atom >= d - 1)
            if way == 0
            else jnp.logical_and(atom > 0, atom + d - 1 < n_atom)
        )
        return jnp.clip(origin, 0, n_atom - 1), able

    filled_of = {0: grid > 0, 1: grid >= 0, 2: grid < n_grid - 1}

    def line_send(slot, d):
        for way in range(2):
            origin, able = line(slot, d, way)

            @pl.when(jnp.logical_and(able, filled_of[slot]))
            def _():
                source = piece if slot == 1 and d == 1 else basis.at[slot, origin]
                send(
                    source, basis.at[slot, origin], line_sent.at[slot, way, d - 1],
                    line_got.at[slot, way, d - 1], (grid, atom + 1 - 2 * way),
                )

    def line_wait(slot, d, sems, arrived):
        for way in range(2):
            if arrived:
                able = atom >= d if way == 0 else atom + d < n_atom
            else:
                able = line(slot, d, way)[1]

            @pl.when(jnp.logical_and(able, filled_of[slot]))
            def _():
                wait_bytes(piece, sems.at[slot, way, d - 1])

    line_send(1, 1)
    basis[1, atom] = piece[...]
    all_names[1] = names[...]
    for slot, _, _, filled in sides:

        @pl.when(filled)
        def _():
            wait_bytes(piece, piece_got.at[slot])

        @pl.when(jnp.logical_not(filled))
        def _():
            all_names[slot] = jnp.full_like(names, -1)

    line_send(0, 1)
    line_send(2, 1)
    moved = 0
    for d in range(1, n_atom):
        for slot in (1, 0, 2):
            line_wait(slot, d, line_got, True)
            if d < n_atom - 1:
                line_send(slot, d + 1)
        while moved < ROUNDS and moved < (d * ROUNDS) // (n_atom - 1):
            halo.forward(moved)
            moved += 1
    for d in range(1, n_atom):
        for slot in (1, 0, 2):
            line_wait(slot, d, line_sent, False)
    for slot, _, able, filled in sides:

        @pl.when(able)
        def _():
            wait_bytes(piece, piece_sent.at[slot])
            wait_bytes(names, name_sent.at[slot])

        @pl.when(filled)
        def _():
            wait_bytes(names, name_got.at[slot])

    halo.finish()


def halo_of(shape, own, piece, names):
    rows, columns = own.shape
    anywhere = pl.BlockSpec(memory_space=pl.ANY)
    return pl.pallas_call(
        functools.partial(halo_kernel, shape),
        out_shape=(
            jax.ShapeDtypeStruct(own.shape, own.dtype),
            jax.ShapeDtypeStruct(own.shape, own.dtype),
            jax.ShapeDtypeStruct((3, shape[1], *piece.shape), piece.dtype),
            jax.ShapeDtypeStruct((3, *names.shape), names.dtype),
            jax.ShapeDtypeStruct((2, rows // 2, columns), own.dtype),
        ),
        in_specs=[anywhere, VMEM, VMEM],
        out_specs=(anywhere, anywhere, VMEM, VMEM, anywhere),
        scratch_shapes=halo_scratch(ROUNDS)
        + [
            pltpu.SemaphoreType.DMA((3,)),
            pltpu.SemaphoreType.DMA((3,)),
            pltpu.SemaphoreType.DMA((3,)),
            pltpu.SemaphoreType.DMA((3,)),
            pltpu.SemaphoreType.DMA((3, 2, shape[1] - 1)),
            pltpu.SemaphoreType.DMA((3, 2, shape[1] - 1)),
        ],
        compiler_params=pltpu.CompilerParams(
            collective_id=1, has_side_effects=True, vmem_limit_bytes=24 << 20
        ),
        name="halo_of",
    )(own, piece, names)


def to_columns(rows):
    parts = [
        jnp.transpose(jnp.broadcast_to(rows[i : i + 1, :], (LANES, LANES)))
        for i in range(rows.shape[0])
    ]
    return jnp.concatenate(parts, axis=0)


def to_rows(columns):
    parts = []
    for i in range(columns.shape[0] // LANES):
        piece = jnp.broadcast_to(columns[i * LANES : (i + 1) * LANES, :], (LANES, LANES))
        parts.append(jnp.transpose(piece)[0:1, :])
    return jnp.concatenate(parts, axis=0)


def psi_kernel(lists, basis_t, below, own, above, psi, dens, rows, sums, basis):
    step = pl.program_id(0)
    owned = own.shape[0]
    rows[0:owned, :] = below[...]
    rows[owned : 2 * owned, :] = own[...]
    rows[2 * owned : 3 * owned, :] = above[...]
    count, points, depth = basis.shape
    picks = lists.shape[1]
    width = depth // picks
    wide = psi.shape[2]

    @pl.when(step == 0)
    def _():
        sums[...] = jnp.zeros_like(sums)
        for b in range(count):
            basis[b] = jnp.transpose(basis_t[0, b])

    @pl.loop(0, count)
    def _(b):
        chosen = jnp.concatenate(
            [
                rows[pl.ds(pl.multiple_of(lists[b, j] * width, width), width), :]
                for j in range(picks)
            ],
            axis=0,
        )
        value = jnp.dot(basis[b], chosen, preferred_element_type=jnp.float32)
        rounded = value.astype(jnp.bfloat16)
        psi[b] = rounded
        square = jnp.square(rounded.astype(jnp.float32))
        total = square[:, 0:LANES]
        for i in range(1, wide // LANES):
            total = total + square[:, i * LANES : (i + 1) * LANES]
        sums[b] += total

    @pl.when(step == pl.num_programs(0) - 1)
    def _():
        for b in range(count):
            dens[b : b + 1, :] = jnp.sum(jnp.transpose(sums[b]), axis=0, keepdims=True)


def psi_and_density(lists, basis_t, below, own, above):
    owned, columns = own.shape
    _, count, depth, points = basis_t.shape
    wide = min(columns, 512)
    grant = 2 * (9 * owned * wide + 2 * count * points * wide + 4 * count * depth * points)
    tile = pl.BlockSpec((owned, wide), lambda i, lists: (0, i))
    return pl.pallas_call(
        psi_kernel,
        out_shape=(
            jax.ShapeDtypeStruct((count, points, columns), jnp.bfloat16),
            jax.ShapeDtypeStruct((count, points), jnp.float32),
        ),
        grid_spec=pltpu.PrefetchScalarGridSpec(
            num_scalar_prefetch=1,
            grid=(columns // wide,),
            in_specs=[
                pl.BlockSpec((1, count, depth, points), lambda i, lists: (1, 0, 0, 0)),
                tile,
                tile,
                tile,
            ],
            out_specs=(
                pl.BlockSpec((count, points, wide), lambda i, lists: (0, 0, i)),
                pl.BlockSpec((count, points), lambda i, lists: (0, 0)),
            ),
            scratch_shapes=[
                pltpu.VMEM((3 * owned, wide), jnp.bfloat16),
                pltpu.VMEM((count, points, LANES), jnp.float32),
                pltpu.VMEM((count, points, depth), jnp.bfloat16),
            ],
        ),
        compiler_params=pltpu.CompilerParams(vmem_limit_bytes=grant + (6 << 20)),
        cost_estimate=pl.CostEstimate(
            flops=2 * count * points * depth * columns,
            bytes_accessed=8 * owned * columns,
            transcendentals=0,
        ),
        name="psi_and_density",
    )(lists, basis_t, below, own, above)


def potential_kernel(
    shape, layers, psi, dens, info, mine, hot, hot_t, weights, scale, shift, mw, aw, head,
    pot, near, psi_low, psi_high, relay,
    dens_buf, info_buf, rows_out, rows_buf, scaled_out, scaled_buf, sent, got,
    psi_sent, psi_got, psi_passed,
):
    n_grid, n_atom = shape
    n = n_grid * n_atom
    grid, atom = lax.axis_index("grid"), lax.axis_index("atom")
    me = grid * n_atom + atom

    def other(d):
        t = lax.rem(me + d, n)
        return (t // n_atom, lax.rem(t, n_atom))

    def to_all(source, held, k):
        @pl.loop(1, n)
        def _(d):
            pltpu.make_async_remote_copy(
                src_ref=source,
                dst_ref=held.at[me],
                send_sem=sent.at[k],
                recv_sem=got.at[k],
                device_id=other(d),
                device_id_type=MESH,
            ).start()

    def wait_all(held, sem, count):
        part = held.at[pl.ds(0, count)]
        pltpu.make_async_copy(part, part, sem).wait()

    meet_all(shape)
    halo = Halo(n_grid, layers + 2, psi, psi_low, psi_high, relay, psi_sent, psi_got, psi_passed)

    @pl.loop(1, n_atom)
    def _(d):
        to = lax.rem(atom + d, n_atom)
        pltpu.make_async_remote_copy(
            src_ref=dens.at[to],
            dst_ref=dens_buf.at[atom],
            send_sem=sent.at[0],
            recv_sem=got.at[0],
            device_id=(grid, to),
            device_id_type=MESH,
        ).start()

    to_all(info, info_buf, 1)
    halo.send(0)
    dens_buf[atom] = dens[atom]
    info_buf[me] = info[...]
    weight = to_columns(weights[...])[:, 0:1]

    wait_all(dens_buf, got.at[0], n_atom - 1)
    density = to_columns(2.0 * jnp.sum(dens_buf[...], axis=0))
    safe = jnp.where(density > 0.0, density, 1.0)
    radius = jnp.where(density > 0.0, jnp.exp(jnp.log(safe) * (1.0 / 3.0)), 0.0)[:, 0:1]
    hidden = jax.nn.silu(radius * scale[...] + shift[...])
    halves = hidden.shape[1] // LANES
    picks = []
    share = None
    for layer in range(layers):
        message = jax.nn.silu(
            jnp.dot(hidden.astype(jnp.bfloat16), mw[layer], preferred_element_type=jnp.float32)
        )
        weighted = (weight * message).astype(jnp.bfloat16)
        part = jnp.dot(hot_t[...], weighted, preferred_element_type=jnp.float32)
        rows_out[layer] = jnp.concatenate(
            [part[0:RUN, h * LANES : (h + 1) * LANES] for h in range(halves)], axis=0
        ).astype(jnp.bfloat16)
        to_all(rows_out.at[layer], rows_buf.at[layer], 2 + layer)
        halo.send(1 + layer)
        rows_buf[layer, me] = rows_out[layer]
        if layer == 0:
            wait_all(info_buf, got.at[1], n - 1)
            facts = info_buf[...].reshape(n * RUN, LANES)
            same = (facts[:, 0:1] == mine[...]).astype(jnp.float32)
            mass = jnp.sum(same * facts[:, LANES // 2 : LANES // 2 + 1], axis=0, keepdims=True)
            share = 1.0 / (1.0 + to_columns(mass)[:, 0:1])
            same = same.reshape(n, RUN, LANES)
            none = jnp.zeros_like(same)
            for h in range(halves):
                full = jnp.concatenate(
                    [same if k == h else none for k in range(halves)], axis=1
                ).reshape(n * RUN * halves, LANES)
                picks.append(jnp.transpose(full).astype(jnp.bfloat16))
        wait_all(rows_buf.at[layer], got.at[2 + layer], n - 1)
        halo.forward(layer)
        held = rows_buf[layer].reshape(n * RUN * halves, LANES)
        rows = jnp.concatenate(
            [jnp.dot(pick, held, preferred_element_type=jnp.float32) for pick in picks], axis=1
        )
        update = jax.nn.silu(
            jnp.dot(
                (rows * share).astype(jnp.bfloat16), aw[layer], preferred_element_type=jnp.float32
            )
        ).astype(jnp.bfloat16)
        picked = jnp.dot(hot[...], update, preferred_element_type=jnp.float32)
        hidden = hidden + message * picked
    score = jnp.sum(hidden * head[...], axis=1, keepdims=True)
    potential = radius * (1.0 + jnp.tanh(score))
    pot[...] = to_rows(potential)
    last = 2 + layers
    scaled_out[...] = to_rows(weight * potential)
    to_all(scaled_out, scaled_buf, last)
    halo.send(layers + 1)
    scaled_buf[me] = scaled_out[...]
    wait_all(scaled_buf, got.at[last], n - 1)
    halo.forward(layers)
    halo.forward(layers + 1)
    for k in range(3):
        group = jnp.clip(grid - 1 + k, 0, n_grid - 1)
        near[k * n_atom : (k + 1) * n_atom] = scaled_buf[pl.ds(group * n_atom, n_atom)]
    wait_all(dens_buf, sent.at[0], n_atom - 1)
    wait_all(info_buf, sent.at[1], n - 1)
    for layer in range(layers):
        wait_all(rows_buf.at[layer], sent.at[2 + layer], n - 1)
    wait_all(scaled_buf, sent.at[last], n - 1)
    halo.finish()


def potential_of(shape, psi, dens, info, mine, hot, hot_t, weights, scale, shift, mw, aw, head):
    n_atom, batches, points = dens.shape
    n = shape[0] * shape[1]
    layers, features, _ = mw.shape
    packed = RUN * (features // LANES)
    anywhere = pl.BlockSpec(memory_space=pl.ANY)
    return pl.pallas_call(
        functools.partial(potential_kernel, shape, layers),
        out_shape=(
            jax.ShapeDtypeStruct((batches, points), jnp.float32),
            jax.ShapeDtypeStruct((3 * n_atom, batches, points), jnp.float32),
            jax.ShapeDtypeStruct(psi.shape, psi.dtype),
            jax.ShapeDtypeStruct(psi.shape, psi.dtype),
            jax.ShapeDtypeStruct((2, psi.shape[0] // 2, *psi.shape[1:]), psi.dtype),
        ),
        in_specs=[anywhere] + [VMEM] * 11,
        out_specs=(VMEM, VMEM, anywhere, anywhere, anywhere),
        scratch_shapes=[
            pltpu.VMEM((n_atom, batches, points), jnp.float32),
            pltpu.VMEM((n, RUN, LANES), jnp.float32),
            pltpu.VMEM((layers, packed, LANES), jnp.bfloat16),
            pltpu.VMEM((layers, n, packed, LANES), jnp.bfloat16),
            pltpu.VMEM((batches, points), jnp.float32),
            pltpu.VMEM((n, batches, points), jnp.float32),
            pltpu.SemaphoreType.DMA((3 + layers,)),
            pltpu.SemaphoreType.DMA((3 + layers,)),
        ]
        + halo_scratch(layers + 2),
        compiler_params=pltpu.CompilerParams(
            collective_id=0, has_side_effects=True, vmem_limit_bytes=24 << 20
        ),
        cost_estimate=pl.CostEstimate(
            flops=20_000_000_000, bytes_accessed=4_000_000, transcendentals=0
        ),
        name="potential_of",
    )(psi, dens, info, mine, hot, hot_t, weights, scale, shift, mw, aw, head)


def fock_kernel(lists, basis_t, near, low, mid, high, out, scaled):
    step = pl.program_id(0)
    groups, count, depth, points = basis_t.shape
    picks = lists.shape[1]
    width = depth // picks
    owned = out.shape[0] // width

    @pl.when(step == 0)
    def _():
        @pl.loop(0, groups)
        def _(k):
            @pl.loop(0, count)
            def _(b):
                scaled[k, b] = (
                    basis_t[k, b].astype(jnp.float32) * near[pl.ds(k * count + b, 1), :]
                ).astype(jnp.bfloat16)

    out[...] = jnp.zeros_like(out)
    for k, psi in enumerate((low, mid, high)):

        @pl.loop(0, count)
        def _(b, k=k, psi=psi):
            for j in range(picks):
                block = lists[k * count + b, j]

                @pl.when(jnp.logical_and(block >= 0, block < owned))
                def _():
                    at = pl.ds(pl.multiple_of(block * width, width), width)
                    out[at, :] += jnp.dot(
                        scaled[k, b, j * width : (j + 1) * width, :],
                        psi[b],
                        preferred_element_type=jnp.float32,
                    )


def fock_of(lists, basis_t, near, low, mid, high, owned):
    groups, count, depth, points = basis_t.shape
    columns = mid.shape[2]
    wide = min(columns, 512)
    tile = pl.BlockSpec((count, points, wide), lambda i, lists: (0, 0, i))
    grant = 2 * (9 * count * depth * points + 6 * count * points * wide + 4 * owned * wide)
    return pl.pallas_call(
        fock_kernel,
        out_shape=jax.ShapeDtypeStruct((owned, columns), jnp.float32),
        grid_spec=pltpu.PrefetchScalarGridSpec(
            num_scalar_prefetch=1,
            grid=(columns // wide,),
            in_specs=[
                pl.BlockSpec((groups, count, depth, points), lambda i, lists: (0, 0, 0, 0)),
                pl.BlockSpec((groups * count, points), lambda i, lists: (0, 0)),
                tile,
                tile,
                tile,
            ],
            out_specs=pl.BlockSpec((owned, wide), lambda i, lists: (0, i)),
            scratch_shapes=[pltpu.VMEM((groups, count, depth, points), jnp.bfloat16)],
        ),
        compiler_params=pltpu.CompilerParams(vmem_limit_bytes=grant + (4 << 20)),
        name="fock_of",
    )(lists, basis_t, near, low, mid, high)


def local(
    basis_values,
    block_lists,
    orbitals,
    point_weights,
    point_atoms,
    embed_scale,
    embed_shift,
    message_weight,
    atom_weight,
    head_weight,
):
    n_grid, n_atom = lax.axis_size("grid"), lax.axis_size("atom")
    own_rows = orbitals.shape[0]
    batches, points, depth = basis_values.shape
    width = depth // block_lists.shape[1]
    owned = own_rows // width
    shape = (n_grid, n_atom)
    first = lax.axis_index("grid") * owned
    names = jnp.pad(block_lists, ((0, 0), (0, LANES - block_lists.shape[1])))
    below, above, basis_t, names, _ = halo_of(
        shape, orbitals, jnp.swapaxes(basis_values, 1, 2), names
    )
    basis_t = basis_t.reshape(3, n_atom * batches, depth, points)
    lists = names[:, :, : block_lists.shape[1]].reshape(-1, block_lists.shape[1]) - first

    total = ATOM_DEV * n_atom
    lead = point_atoms[0]
    shifted = (point_atoms - lead + total // 2) % total - total // 2
    least = jnp.min(shifted)
    start = (lead + least) % total
    place = shifted - least
    lanes = jnp.arange(LANES, dtype=jnp.int32)
    onehot = place[:, None] == lanes[None, :]
    hot = onehot.astype(jnp.bfloat16)
    hot_t = (place[None, :] == lanes[:, None]).astype(jnp.bfloat16)
    mass = jnp.sum(jnp.where(onehot, point_weights[:, None], 0.0), axis=0)[:RUN]
    names = ((start + lanes) % total).astype(jnp.float32)
    mine = jnp.where(lanes < RUN, names, -1.0)[None, :]
    info = jnp.where(lanes[None, :] < LANES // 2, names[:RUN, None], mass[:, None])

    psi, dens = psi_and_density(block_lists - first + owned, basis_t, below, orbitals, above)
    potential, near, psi_low, psi_high, _ = potential_of(
        shape,
        psi,
        dens.reshape(n_atom, batches, points),
        info,
        mine,
        hot,
        hot_t,
        point_weights.reshape(batches, points),
        embed_scale[None, :],
        embed_shift[None, :],
        message_weight,
        atom_weight,
        head_weight[None, :],
    )
    fock = fock_of(
        lists, basis_t, near.reshape(-1, points), psi_low, psi, psi_high, own_rows
    )
    return (fock, potential.reshape(-1))


def solution(mesh):
    return jax.shard_map(
        local,
        mesh=mesh,
        in_specs=(
            P(("grid", "atom"), None, None),
            P("grid", None),
            P("grid", "atom"),
            P(("grid", "atom")),
            P(("grid", "atom")),
            P(),
            P(),
            P(),
            P(),
            P(),
        ),
        out_specs=(P("grid", "atom"), P(("grid", "atom"))),
        check_vma=False,
    )
```

profile of v0, /device:TPU:1, one launch (start us, length us, event | category | flops | bytes accessed | tf_op | source)
XLA Modules:
  0.0 142.5 jit_solution(11056430502375952635)
XLA Ops:
  0.6 1.2 slice.13
  1.8 2.0 %fusion.8 = (s32[]{:T(128)}, s32[256]{0:T(256)S(1)}) fusion(s32[256]{0:T(256)} %param.14, s32[]{:T(128)} %bitcast.4), kind=kLoop, calls=%fused_computation.26 | loop fusion | flops 3839 | bytes 2056 | tf_op jit(solution)/shard_map/reduce_min | solution.py:605
  5.1 0.7 broadcast_subtract_fusion
  5.8 0.8 select_reduce_fusion
  6.6 0.1 broadcast_select_fusion.info
  6.7 0.8 copy.18
  7.5 0.1 fusion.hot
  7.6 1.1 copy.17
  8.7 0.0 copy-start
  8.7 1.9 %copy-done = bf16[1536,1024]{1,0:T(8,128)(2,1)S(1)} copy-done((bf16[1536,1024]{1,0:T(8,128)(2,1)S(1)}, bf16[1536,1024]{1,0:T(8,128)(2,1)}, u32[]{:S(2)}) %copy-start) | copy-done | bytes 3145752
  10.6 0.0 copy-start.1
  10.6 64.9 %halo_of.1 = (bf16[1536,1024]{1,0:T(8,128)(2,1)S(1)}, bf16[1536,1024]{1,0:T(8,128)(2,1)S(1)}, bf16[3,4,2,512,128]{4,3,2,1,0:T(8,128)(2,1)S(1)}, s32[3,8,128]{2,1,0:T(8,128)S(1)}, bf16[2,768,1024]{2,1,0:T(8,128)(2,1)}) custom-call(bf16[1536,1024]{1,0:T(8,128)(2,1)S(1)} %copy-done, bf16[2,512,128]{2,1,0:T(8,128)(2,1)S(1)} %bitcast.16, s32[8,128]{1,0:T(8,128)S(1)} %pad.4.names), custom_call_target="tpu_custom_call" | custom-call | tf_op jit(solution)/shard_map/halo_of/pallas_call | solution.py:231
  75.6 0.0 copy-done.1
  75.6 0.0 copy-start.2
  75.6 0.0 copy-start.3
  75.6 0.0 copy-start.4
  75.6 0.0 copy-start.5
  75.6 0.0 copy-start.6
  75.6 0.0 copy-start.7
  75.6 6.6 %psi_and_density.1 = (bf16[8,128,1024]{2,1,0:T(8,128)(2,1)S(1)}, f32[8,128]{1,0:T(8,128)S(1)}) custom-call(s32[8,4]{1,0:T(8,128)S(1)} %subtract_add_fusion.lists, bf16[3,8,512,128]{3,2,1,0:T(8,128)(2,1)S(1)} %bitcast.14, bf16[1536,1024]{1,0:T(8,128)(2,1)S(1)} %get-tuple-element.14.below, bf16[1536,1024]{1,0:T(8,128)(2,1)S(1)} %copy-done.1, ...), custom_call_target="tpu_custom_call" | custom-call | flops 1073741824 | bytes 12582912 | tf_op jit(solution)/shard_map/psi_and_density/pallas_call | solution.py:321
  82.2 0.0 copy-done.2
  82.2 0.0 copy-done.3
  82.2 0.0 copy-done.4
  82.2 0.0 copy-done.5
  82.3 0.0 copy-done.6
  82.3 0.0 copy-done.7
  82.3 42.1 %potential_of.1 = (f32[2,128]{1,0:T(2,128)S(1)}, f32[12,2,128]{2,1,0:T(2,128)S(1)}, bf16[8,128,1024]{2,1,0:T(8,128)(2,1)S(1)}, bf16[8,128,1024]{2,1,0:T(8,128)(2,1)S(1)}, bf16[2,4,128,1024]{3,2,1,0:T(8,128)(2,1)}) custom-call(bf16[8,128,1024]{2,1,0:T(8,128)(2,1)S(1)} %get-tuple-element.16.psi.mid, f32[4,2,128]{2,1,0:T(2,128)S(1)} %bitcast.20, ...), custom_call_target="tpu_custom_call" | custom-call | flops 20000000000 | bytes 4000000 | tf_op jit(solution)/shard_map/potential_of/pallas_call | solution.py:482
  124.4 17.5 %fock_of.1 = f32[1536,1024]{1,0:T(8,128)} custom-call(s32[24,4]{1,0:T(8,128)S(1)} %subtract_bitcast_fusion.lists, bf16[3,8,512,128]{3,2,1,0:T(8,128)(2,1)S(1)} %bitcast.15, f32[24,128]{1,0:T(8,128)S(1)} %bitcast.17, bf16[8,128,1024]{2,1,0:T(8,128)(2,1)S(1)} %get-tuple-element.19.low, bf16[8,128,1024]{2,1,0:T(8,128)(2,1)S(1)} %get-tuple-element.16.psi.mid, ...), custom_call_target="tpu_custom_call" | custom-call | tf_op jit(solution)/shard_map/fock_of/pallas_call | solution.py:555
  141.9 0.6 copy.24
  (7 shorter events, 0.1 us)
Async XLA Ops:
  8.7 1.9 %copy-start = (bf16[1536,1024]{1,0:T(8,128)(2,1)S(1)}, bf16[1536,1024]{1,0:T(8,128)(2,1)}, u32[]{:S(2)}) copy-start(bf16[1536,1024]{1,0:T(8,128)(2,1)} %own.3) | copy-start | bytes 9437188
  10.6 64.9 %copy-start.1 = (bf16[1536,1024]{1,0:T(8,128)(2,1)S(1)}, bf16[1536,1024]{1,0:T(8,128)(2,1)}, u32[]{:S(2)}) copy-start(bf16[1536,1024]{1,0:T(8,128)(2,1)} %own.3) | copy-start | bytes 9437188
  75.6 6.7 %copy-start.2 = (f32[256]{0:T(256)S(1)}, f32[256]{0:T(256)}, u32[]{:S(2)}) copy-start(f32[256]{0:T(256)} %param.13) | copy-start | bytes 3076
  75.6 6.6 %copy-start.3 = (bf16[2,256,256]{2,1,0:T(8,128)(2,1)S(1)}, bf16[2,256,256]{2,1,0:T(8,128)(2,1)}, u32[]{:S(2)}) copy-start(bf16[2,256,256]{2,1,0:T(8,128)(2,1)} %mw.1) | copy-start | bytes 786436
  75.6 6.6 %copy-start.4 = (bf16[2,256,256]{2,1,0:T(8,128)(2,1)S(1)}, bf16[2,256,256]{2,1,0:T(8,128)(2,1)}, u32[]{:S(2)}) copy-start(bf16[2,256,256]{2,1,0:T(8,128)(2,1)} %aw.1) | copy-start | bytes 786436
  75.6 6.6 %copy-start.5 = (f32[256]{0:T(256)S(1)}, f32[256]{0:T(256)}, u32[]{:S(2)}) copy-start(f32[256]{0:T(256)} %param.15) | copy-start | bytes 3076
  75.6 6.6 %copy-start.6 = (f32[256]{0:T(256)S(1)}, f32[256]{0:T(256)}, u32[]{:S(2)}) copy-start(f32[256]{0:T(256)} %param.16) | copy-start | bytes 3076
  75.6 6.6 %copy-start.7 = (f32[256]{0:T(256)S(1)}, f32[256]{0:T(256)}, u32[]{:S(2)}) copy-start(f32[256]{0:T(256)} %param.19) | copy-start | bytes 3076
where the time goes:
time: 144 us; the launch traced here: 142 us
  Pallas kernels  131 us (91%)
  local copies, waits for them, and re-layouts  5.56 us (4%)
  other arithmetic  3.67 us (3%)
  between operations  2.13 us (1%)
    pallas_call x1, Pallas kernels, halo_of(): pl.pallas_call(functools.partial(halo_kernel, shape), out_shape=(jax.Shap...  64.9 us
    pallas_call x1, Pallas kernels, potential_of(): pl.pallas_call(functools.partial(potential_kernel, shape, layers), out_sh...  42.1 us
    pallas_call x1, Pallas kernels, fock_of(): pl.pallas_call(fock_kernel, out_shape=jax.ShapeDtypeStruct((owned, column...  17.5 us
    pallas_call x1, Pallas kernels, psi_and_density(): pl.pallas_call(psi_kernel, out_shape=(jax.ShapeDtypeStruct((count, points...  6.57 us
    unnamed x19, local copies, waits for them, and re-layouts  4.37 us

commit v1 on v0

v1 whole, which is shorter than its diff:
```python
import functools
import jax
import jax.numpy as jnp
from jax import lax
from jax.experimental import pallas as pl
from jax.experimental.pallas import tpu as pltpu
from jax.sharding import PartitionSpec as P

ATOM_DEV = 32
RUN = max(ATOM_DEV // 4, 1)
LANES = 128
VMEM = pl.BlockSpec(memory_space=pltpu.VMEM)
HBM = pl.BlockSpec(memory_space=pltpu.HBM)
MESH = pl.DeviceIdType.MESH
TILE = 256


def wait_bytes(ref, sem):
    pltpu.make_async_copy(ref, ref, sem).wait()


def meet_all(shape):
    n_grid, n_atom = shape
    n = n_grid * n_atom
    me = lax.axis_index("grid") * n_atom + lax.axis_index("atom")
    barrier = pltpu.get_barrier_semaphore()

    @pl.loop(1, n)
    def _(d):
        t = lax.rem(me + d, n)
        pl.semaphore_signal(
            barrier, inc=1, device_id=(t // n_atom, lax.rem(t, n_atom)), device_id_type=MESH
        )

    pl.semaphore_wait(barrier, n - 1)


def to_columns(rows):
    parts = [
        jnp.transpose(jnp.broadcast_to(rows[i : i + 1, :], (LANES, LANES)))
        for i in range(rows.shape[0])
    ]
    return jnp.concatenate(parts, axis=0)


def to_rows(columns):
    parts = []
    for i in range(columns.shape[0] // LANES):
        piece = jnp.broadcast_to(columns[i * LANES : (i + 1) * LANES, :], (LANES, LANES))
        parts.append(jnp.transpose(piece)[0:1, :])
    return jnp.concatenate(parts, axis=0)


def wrapped(values, total):
    values = jnp.where(values < 0.0, values + total, values)
    return jnp.where(values >= total, values - total, values)


def exchange_kernel(
    shape, layers, own, piece, names, atoms, weights, scale, shift, mw_in, aw_in, head,
    pot, near, psi, basis_t, all_names,
    rows, basis, lists, acc, part_out, part_in, relay, mw, aw, dens, dens_buf,
    info, info_buf, rows_out, rows_buf, scaled_out, scaled_buf,
    load, list_sem, name_sent, name_got, v_sent, v_got, z_sent, chip_sent,
    part_sent, part_got, psi_sent, psi_got, passed, relay_sent, sent, got,
):
    n_grid, n_atom = shape
    n = n_grid * n_atom
    grid, atom = lax.axis_index("grid"), lax.axis_index("atom")
    me = grid * n_atom + atom
    last, middle = n_grid - 1, n_grid // 2
    side = lax.rem(grid, 2)
    outer, inner = 2 * side, 2 - 2 * side
    og, ig = grid - 1 + 2 * side, grid + 1 - 2 * side
    has_outer = jnp.logical_and(og >= 0, og < n_grid)
    at_split = jnp.logical_or(grid == middle - 1, grid == middle)
    whole = jnp.logical_and(has_outer, jnp.logical_not(at_split))
    relays = jnp.logical_or(grid == 0, grid == last)
    relay_to = jnp.where(grid == middle, 0, last)
    forward_to = jnp.where(grid == 0, middle - 1, middle)

    nb, points, depth = piece.shape
    owned, width, columns = own.shape
    picks = depth // width
    tile = min(columns, TILE)
    relayed = nb // 2
    direct = nb - relayed

    def remote(source, target, send_sem, recv_sem, to):
        pltpu.make_async_remote_copy(
            src_ref=source,
            dst_ref=target,
            send_sem=send_sem,
            recv_sem=recv_sem,
            device_id=to,
            device_id_type=MESH,
        ).start()

    def to_all(source, held, k):
        @pl.loop(1, n)
        def _(d):
            t = lax.rem(me + d, n)
            remote(
                source, held.at[me], sent.at[k], got.at[k],
                (t // n_atom, lax.rem(t, n_atom)),
            )

    def wait_all(held, sem, count):
        wait_bytes(held.at[pl.ds(0, count)], sem)

    def visit(t):
        reach = jnp.minimum(atom, n_atom - 1 - atom)
        close = jnp.where(lax.rem(t, 2) == 1, atom - (t + 1) // 2, atom + t // 2)
        far = jnp.where(reach == atom, t, n_atom - 1 - t)
        return jnp.where(t <= 2 * reach, close, far)

    loads = [
        pltpu.make_async_copy(own, rows.at[pl.ds(1, owned)], load.at[0]),
        pltpu.make_async_copy(mw_in, mw, load.at[1]),
        pltpu.make_async_copy(aw_in, aw, load.at[2]),
    ]
    for copy in loads:
        copy.start()
    meet_all(shape)

    @pl.when(has_outer)
    def _():
        remote(names, all_names.at[inner], name_sent.at[0], name_got.at[inner], (og, atom))
        remote(piece, basis.at[inner, atom], v_sent.at[0], v_got.at[inner, atom], (og, atom))

    remote(names, all_names.at[outer], name_sent.at[1], name_got.at[outer], (ig, atom))
    remote(piece, basis.at[outer, atom], v_sent.at[1], v_got.at[outer, atom], (ig, atom))

    @pl.when(atom < n_atom - 1)
    def _():
        remote(
            piece, basis.at[1, atom], z_sent.at[0, 0, atom], v_got.at[1, atom], (grid, atom + 1)
        )

    @pl.when(atom > 0)
    def _():
        remote(
            piece, basis.at[1, atom], z_sent.at[0, 1, atom], v_got.at[1, atom], (grid, atom - 1)
        )

    total = float(ATOM_DEV * n_atom)
    named = atoms[...].astype(jnp.float32)
    lead = named[0:1, 0:1]
    shifted = wrapped(named - lead + total / 2, total) - total / 2
    least = jnp.min(jnp.min(shifted, axis=1, keepdims=True), axis=0, keepdims=True)
    start = wrapped(lead + least, total)
    place = shifted - least
    lane = lax.broadcasted_iota(jnp.int32, (1, LANES), 1)
    mine = jnp.where(lane < RUN, wrapped(start + lane.astype(jnp.float32), total), -1.0)
    run = lax.broadcasted_iota(jnp.int32, (RUN, LANES), 0).astype(jnp.float32)
    mass = jnp.zeros((RUN, 1), jnp.float32)
    for i in range(nb):
        here = jnp.where(place[i : i + 1, :] == run, weights[i : i + 1, :], 0.0)
        mass = mass + jnp.sum(here, axis=1, keepdims=True)
    info[...] = jnp.where(
        lax.broadcasted_iota(jnp.int32, (RUN, LANES), 1) < LANES // 2,
        wrapped(start + run, total),
        mass,
    )
    to_all(info, info_buf, 1)
    info_buf[me] = info[...]

    basis[1, atom] = piece[...]
    all_names[1] = names[...]
    for edge in (0, owned + 1):
        rows[edge] = jnp.zeros((width, columns), rows.dtype)

    @pl.when(jnp.logical_not(has_outer))
    def _():
        all_names[outer] = jnp.full_like(names, -1)
        part_in[0] = jnp.zeros(part_in.shape[1:], part_in.dtype)

    @pl.when(has_outer)
    def _():
        wait_bytes(names, name_got.at[outer])

    wait_bytes(names, name_got.at[inner])
    copy = pltpu.make_async_copy(all_names, lists, list_sem.at[0])
    copy.start()
    copy.wait()
    loads[0].wait()
    first = grid * owned

    def product(slot, q, i, keep):
        chosen = []
        for j in range(picks):
            block = lists[slot, q * nb + i, j] - first + 1
            chosen.append(jnp.minimum(jnp.maximum(block, 0), owned + 1))
        values = basis[slot, q, i]
        for c in range(columns // tile):
            at = pl.ds(c * tile, tile)
            held = jnp.concatenate(
                [rows[k, :, at] for k in chosen], axis=0
            )
            keep(at, jnp.dot(values, held, preferred_element_type=jnp.float32))

    def outward(phase, q, i, source, target, sent_sem, got_sem):
        @pl.when(whole)
        def _():
            remote(source, target, sent_sem, got_sem, (og, atom))

        if i < direct:

            @pl.when(at_split)
            def _():
                remote(source, target, sent_sem, got_sem, (og, atom))
        else:

            @pl.when(at_split)
            def _():
                remote(
                    source, relay.at[phase, q, i - direct], sent_sem, passed.at[phase, q],
                    (relay_to, atom),
                )

    def forward(phase, r):
        q = visit(r)

        @pl.when(relays)
        def _():
            held = relay.at[phase, q]
            wait_bytes(held, passed.at[phase, q])
            at = pl.ds(q * nb + direct, relayed)
            if phase == 0:
                target, got_sem = part_in.at[0, at], part_got.at[0, q]
            else:
                target, got_sem = psi.at[inner, at], psi_got.at[inner, q]
            remote(held, target, relay_sent.at[phase], got_sem, (forward_to, atom))

    def finish(q):
        wait_bytes(part_in.at[1, pl.ds(q * nb, nb)], part_got.at[1, q])

        @pl.when(has_outer)
        def _():
            wait_bytes(part_in.at[0, pl.ds(q * nb, nb)], part_got.at[0, q])

        for i in range(nb):
            b = q * nb + i
            sums = jnp.zeros((points, LANES), jnp.float32)
            for c in range(columns // LANES):
                at = pl.ds(c * LANES, LANES)
                value = (
                    acc[b, :, at]
                    + part_in[0, b, :, at].astype(jnp.float32)
                    + part_in[1, b, :, at].astype(jnp.float32)
                )
                rounded = value.astype(jnp.bfloat16)
                psi[1, b, :, at] = rounded
                sums = sums + jnp.square(rounded.astype(jnp.float32))
            dens[q, i : i + 1, :] = jnp.sum(jnp.transpose(sums), axis=0, keepdims=True)

        @pl.when(q != atom)
        def _():
            remote(dens.at[q], dens_buf.at[atom], sent.at[0], got.at[0], (grid, q))

        at = pl.ds(q * nb, nb)
        remote(psi.at[1, at], psi.at[outer, at], psi_sent.at[1], psi_got.at[outer, q], (ig, atom))

    def psi_round(r):
        q = visit(r)
        for i in range(nb):
            b = q * nb + i
            outward(
                1, q, i, psi.at[1, b], psi.at[inner, b], psi_sent.at[0], psi_got.at[inner, q]
            )

    @pl.loop(0, n_atom)
    def _(t):
        q = visit(t)

        @pl.when(t > 0)
        def _():
            wait_bytes(piece, v_got.at[1, q])
            remote(
                basis.at[1, q], basis.at[outer, q], chip_sent.at[q], v_got.at[outer, q],
                (ig, atom),
            )

        def along(stream, slot):
            for way in range(2):
                able = (
                    jnp.logical_and(q <= atom, atom < n_atom - 1)
                    if way == 0
                    else jnp.logical_and(q >= atom, atom > 0)
                )

                @pl.when(able)
                def _():
                    remote(
                        basis.at[slot, q], basis.at[slot, q], z_sent.at[stream, way, q],
                        v_got.at[slot, q], (grid, atom + 1 - 2 * way),
                    )

        @pl.when(has_outer)
        def _():
            wait_bytes(piece, v_got.at[outer, q])
            along(1, outer)

        @pl.when(t > 0)
        def _():
            along(0, 1)

        @pl.when(has_outer)
        def _():
            for i in range(nb):
                b = q * nb + i

                def keep(at, value):
                    part_out[0, b, :, at] = value.astype(jnp.bfloat16)

                product(outer, q, i, keep)
                outward(
                    0, q, i, part_out.at[0, b], part_in.at[0, b], part_sent.at[0],
                    part_got.at[0, q],
                )

        wait_bytes(piece, v_got.at[inner, q])
        for i in range(nb):
            b = q * nb + i

            def keep(at, value):
                part_out[1, b, :, at] = value.astype(jnp.bfloat16)

            product(inner, q, i, keep)
            remote(
                part_out.at[1, b], part_in.at[1, b], part_sent.at[1], part_got.at[1, q],
                (ig, atom),
            )

        for i in range(nb):
            b = q * nb + i

            def keep(at, value):
                acc[b, :, at] = value

            product(1, q, i, keep)
            for slot in range(3):
                basis_t[slot, b] = jnp.transpose(basis[slot, q, i])

        @pl.when(t >= 1)
        def _():
            forward(0, t - 1)

        @pl.when(t >= 2)
        def _():
            finish(visit(t - 2))

    stops = layers + 2

    def rounds(s, act):
        for r in range(n_atom):
            if r * stops // n_atom == s:
                act(r)

    if n_atom < 3:
        finish(visit(0))
    rounds(0, psi_round)
    if n_atom >= 3:
        finish(visit(n_atom - 2))
    forward(0, n_atom - 1)
    finish(visit(n_atom - 1))
    dens_buf[atom] = dens[atom]

    weight = to_columns(weights[...])[:, 0:1]
    spot = to_columns(place)
    hot = (spot == lax.broadcasted_iota(jnp.int32, spot.shape, 1).astype(jnp.float32)).astype(
        jnp.bfloat16
    )
    deep = lax.broadcasted_iota(jnp.int32, (LANES, LANES), 0).astype(jnp.float32)
    hot_t = jnp.concatenate([place[i : i + 1, :] == deep for i in range(nb)], axis=1).astype(
        jnp.bfloat16
    )
    loads[1].wait()
    loads[2].wait()
    halves = scale.shape[1] // LANES
    wait_all(info_buf, got.at[1], n - 1)
    facts = info_buf[...].reshape(n * RUN, LANES)
    same = (facts[:, 0:1] == mine).astype(jnp.float32)
    mass = jnp.sum(same * facts[:, LANES // 2 : LANES // 2 + 1], axis=0, keepdims=True)
    share = 1.0 / (1.0 + to_columns(mass)[:, 0:1])
    same = same.reshape(n, RUN, LANES)
    none = jnp.zeros_like(same)
    selects = []
    for h in range(halves):
        full = jnp.concatenate(
            [same if k == h else none for k in range(halves)], axis=1
        ).reshape(n * RUN * halves, LANES)
        selects.append(jnp.transpose(full).astype(jnp.bfloat16))

    wait_all(dens_buf, got.at[0], n_atom - 1)
    density = to_columns(2.0 * jnp.sum(dens_buf[...], axis=0))
    safe = jnp.where(density > 0.0, density, 1.0)
    radius = jnp.where(density > 0.0, jnp.exp(jnp.log(safe) * (1.0 / 3.0)), 0.0)[:, 0:1]
    hidden = jax.nn.silu(radius * scale[...] + shift[...])
    for layer in range(layers):
        message = jax.nn.silu(
            jnp.dot(hidden.astype(jnp.bfloat16), mw[layer], preferred_element_type=jnp.float32)
        )
        weighted = (weight * message).astype(jnp.bfloat16)
        part = jnp.dot(hot_t, weighted, preferred_element_type=jnp.float32)
        rows_out[layer] = jnp.concatenate(
            [part[0:RUN, h * LANES : (h + 1) * LANES] for h in range(halves)], axis=0
        ).astype(jnp.bfloat16)
        to_all(rows_out.at[layer], rows_buf.at[layer], 2 + layer)
        rounds(1 + layer, psi_round)
        rows_buf[layer, me] = rows_out[layer]
        wait_all(rows_buf.at[layer], got.at[2 + layer], n - 1)
        rounds(layer, functools.partial(forward, 1))
        held = rows_buf[layer].reshape(n * RUN * halves, LANES)
        summed = jnp.concatenate(
            [jnp.dot(pick, held, preferred_element_type=jnp.float32) for pick in selects], axis=1
        )
        update = jax.nn.silu(
            jnp.dot(
                (summed * share).astype(jnp.bfloat16), aw[layer],
                preferred_element_type=jnp.float32,
            )
        ).astype(jnp.bfloat16)
        picked = jnp.dot(hot, update, preferred_element_type=jnp.float32)
        hidden = hidden + message * picked
    score = jnp.sum(hidden * head[...], axis=1, keepdims=True)
    potential = radius * (1.0 + jnp.tanh(score))
    pot[...] = to_rows(potential)
    final = 2 + layers
    scaled_out[...] = to_rows(weight * potential)
    to_all(scaled_out, scaled_buf, final)
    rounds(layers + 1, psi_round)
    scaled_buf[me] = scaled_out[...]
    wait_all(scaled_buf, got.at[final], n - 1)
    rounds(layers, functools.partial(forward, 1))
    rounds(layers + 1, functools.partial(forward, 1))
    for k in range(3):
        group = jnp.clip(grid - 1 + k, 0, n_grid - 1)
        near[k * n_atom : (k + 1) * n_atom] = scaled_buf[pl.ds(group * n_atom, n_atom)]

    @pl.loop(0, n_atom)
    def _(q):
        at = pl.ds(q * nb, nb)
        wait_bytes(psi.at[inner, at], psi_got.at[inner, q])

        @pl.when(has_outer)
        def _():
            wait_bytes(psi.at[outer, at], psi_got.at[outer, q])

        @pl.when(q != atom)
        def _():
            wait_bytes(piece, chip_sent.at[q])

        for way in range(2):
            able = (
                jnp.logical_and(q <= atom, atom < n_atom - 1)
                if way == 0
                else jnp.logical_and(q >= atom, atom > 0)
            )

            @pl.when(able)
            def _():
                wait_bytes(piece, z_sent.at[0, way, q])

            @pl.when(jnp.logical_and(able, has_outer))
            def _():
                wait_bytes(piece, z_sent.at[1, way, q])

    @pl.when(has_outer)
    def _():
        wait_bytes(names, name_sent.at[0])
        wait_bytes(piece, v_sent.at[0])
        wait_bytes(part_out.at[0], part_sent.at[0])
        wait_bytes(psi.at[1], psi_sent.at[0])

    wait_bytes(names, name_sent.at[1])
    wait_bytes(piece, v_sent.at[1])
    wait_bytes(part_out.at[1], part_sent.at[1])
    wait_bytes(psi.at[1], psi_sent.at[1])

    @pl.when(relays)
    def _():
        for phase in range(2):
            wait_bytes(relay.at[phase], relay_sent.at[phase])

    wait_all(dens_buf, sent.at[0], n_atom - 1)
    wait_all(info_buf, sent.at[1], n - 1)
    for layer in range(layers):
        wait_all(rows_buf.at[layer], sent.at[2 + layer], n - 1)
    wait_all(scaled_buf, sent.at[final], n - 1)


def exchange_of(shape, own, piece, names, atoms, weights, scale, shift, mw, aw, head):
    n_grid, n_atom = shape
    n = n_grid * n_atom
    nb, points, depth = piece.shape
    count = nb * n_atom
    width, columns = own.shape[1:]
    layers, features, _ = mw.shape
    packed = RUN * (features // LANES)
    bf16, f32 = jnp.bfloat16, jnp.float32
    dma = pltpu.SemaphoreType.DMA
    grant = 2 * own.size + 14 * count * points * columns + 6 * count * depth * points
    grant += n * (packed * LANES * (2 * layers + 8) + 12 * RUN * LANES) + (6 << 20)
    given = 6 * count * points * (columns + depth)
    if grant + given > 48 << 20:
        grant = 60 << 20
    return pl.pallas_call(
        functools.partial(exchange_kernel, shape, layers),
        out_shape=(
            jax.ShapeDtypeStruct((nb, points), f32),
            jax.ShapeDtypeStruct((3 * n_atom, nb, points), f32),
            jax.ShapeDtypeStruct((3, count, points, columns), bf16),
            jax.ShapeDtypeStruct((3, count, depth, points), bf16),
            jax.ShapeDtypeStruct((3, *names.shape), names.dtype),
        ),
        in_specs=[HBM] + [VMEM] * 6 + [HBM, HBM, VMEM],
        out_specs=(VMEM,) * 5,
        scratch_shapes=[
            pltpu.VMEM((own.shape[0] + 2, width, columns), bf16),
            pltpu.VMEM((3, n_atom, nb, points, depth), bf16),
            pltpu.SMEM((3, *names.shape), names.dtype),
            pltpu.VMEM((count, points, columns), f32),
            pltpu.VMEM((2, count, points, columns), bf16),
            pltpu.VMEM((2, count, points, columns), bf16),
            pltpu.VMEM((2, n_atom, nb // 2, points, columns), bf16),
            pltpu.VMEM(mw.shape, bf16),
            pltpu.VMEM(aw.shape, bf16),
            pltpu.VMEM((n_atom, nb, points), f32),
            pltpu.VMEM((n_atom, nb, points), f32),
            pltpu.VMEM((RUN, LANES), f32),
            pltpu.VMEM((n, RUN, LANES), f32),
            pltpu.VMEM((layers, packed, LANES), bf16),
            pltpu.VMEM((layers, n, packed, LANES), bf16),
            pltpu.VMEM((nb, points), f32),
            pltpu.VMEM((n, nb, points), f32),
            dma((3,)),
            dma((1,)),
            dma((2,)),
            dma((3,)),
            dma((2,)),
            dma((3, n_atom)),
            dma((2, 2, n_atom)),
            dma((n_atom,)),
            dma((2,)),
            dma((2, n_atom)),
            dma((2,)),
            dma((3, n_atom)),
            dma((2, n_atom)),
            dma((2,)),
            dma((3 + layers,)),
            dma((3 + layers,)),
        ],
        compiler_params=pltpu.CompilerParams(
            collective_id=0, has_side_effects=True, vmem_limit_bytes=grant
        ),
        name="exchange_of",
    )(own, piece, names, atoms, weights, scale, shift, mw, aw, head)


def fock_kernel(lists, basis_t, near, psi, out, scaled):
    step = pl.program_id(0)
    groups, count, depth, points = basis_t.shape
    picks = lists.shape[1]
    width = depth // picks
    wide = out.shape[1]
    owned = out.shape[0] // width
    columns = pl.ds(pl.multiple_of(step * wide, wide), wide)

    out[...] = jnp.zeros_like(out)

    @pl.loop(0, groups * count)
    def _(s):
        k, b = s // count, lax.rem(s, count)
        for j in range(picks):
            block = lists[s, j]

            @pl.when(jnp.logical_and(block >= 0, block < owned))
            def _():
                part = slice(j * width, (j + 1) * width)

                @pl.when(step == 0)
                def _():
                    scaled[s, part, :] = (
                        basis_t[k, b, part, :].astype(jnp.float32) * near[pl.ds(s, 1), :]
                    ).astype(jnp.bfloat16)

                at = pl.ds(pl.multiple_of(block * width, width), width)
                out[at, :] += jnp.dot(
                    scaled[s, part, :], psi[k, b, :, columns], preferred_element_type=jnp.float32
                )


def fock_of(lists, basis_t, near, psi, owned):
    groups, count, depth, points = basis_t.shape
    columns = psi.shape[3]
    wide = min(columns, 256)
    grant = 2 * (9 * count * depth * points + 6 * count * points * wide + 4 * owned * wide)
    return pl.pallas_call(
        fock_kernel,
        out_shape=jax.ShapeDtypeStruct((owned, columns), jnp.float32),
        grid_spec=pltpu.PrefetchScalarGridSpec(
            num_scalar_prefetch=1,
            grid=(columns // wide,),
            in_specs=[VMEM, VMEM, VMEM],
            out_specs=pl.BlockSpec((owned, wide), lambda i, lists: (0, i)),
            scratch_shapes=[pltpu.VMEM((groups * count, depth, points), jnp.bfloat16)],
        ),
        compiler_params=pltpu.CompilerParams(vmem_limit_bytes=grant + (12 << 20)),
        name="fock_of",
    )(lists, basis_t, near, psi)


def local(
    basis_values,
    block_lists,
    orbitals,
    point_weights,
    point_atoms,
    embed_scale,
    embed_shift,
    message_weight,
    atom_weight,
    head_weight,
):
    n_grid, n_atom = lax.axis_size("grid"), lax.axis_size("atom")
    own_rows = orbitals.shape[0]
    batches, points, depth = basis_values.shape
    picks = block_lists.shape[1]
    owned = own_rows // (depth // picks)
    first = lax.axis_index("grid") * owned
    names = jnp.pad(block_lists, ((0, 0), (0, LANES - picks)))
    potential, near, psi, basis_t, names = exchange_of(
        (n_grid, n_atom),
        orbitals.reshape(owned, own_rows // owned, -1),
        basis_values,
        names,
        point_atoms.reshape(batches, points),
        point_weights.reshape(batches, points),
        embed_scale[None, :],
        embed_shift[None, :],
        message_weight,
        atom_weight,
        head_weight[None, :],
    )
    lists = names[:, :, :picks].reshape(-1, picks) - first
    fock = fock_of(lists, basis_t, near.reshape(-1, points), psi, own_rows)
    return (fock, potential.reshape(-1))


def solution(mesh):
    return jax.shard_map(
        local,
        mesh=mesh,
        in_specs=(
            P(("grid", "atom"), None, None),
            P("grid", None),
            P("grid", "atom"),
            P(("grid", "atom")),
            P(("grid", "atom")),
            P(),
            P(),
            P(),
            P(),
            P(),
        ),
        out_specs=(P("grid", "atom"), P(("grid", "atom"))),
        check_vma=False,
    )
```

time: 144 us -> 138 us (0.958)
  Pallas kernels: 131 us -> 126 us
  local copies, waits for them, and re-layouts: 5.56 us -> 9.46 us
  other arithmetic: 3.67 us -> 0.01 us
  between operations: 2.13 us -> 0.66 us
    pallas_call x3 -> x1, Pallas kernels: 114 us -> 97.3 us  [exchange_of(): pl.pallas_call(functools.partial(exchange_kernel, shape, layers), out_sha...]
    pallas_call x1, Pallas kernels: 17.5 us -> 29 us  [fock_of(): pl.pallas_call(fock_kernel, out_shape=jax.ShapeDtypeStruct((owned, column...]
    unnamed x19 -> x20, local copies, waits for them, and re-layouts: 4.37 us -> 9.45 us
    reduce_min x1 -> x0, other arithmetic: 1.97 us -> none  [local(): least = jnp.min(shifted)]
where the time goes in v1:
time: 138 us; the launch traced here: 136 us
  Pallas kernels  126 us (91%)
  local copies, waits for them, and re-layouts  9.46 us (7%)
    pallas_call x1, Pallas kernels, exchange_of(): pl.pallas_call(functools.partial(exchange_kernel, shape, layers), out_sha...  97.3 us
    pallas_call x1, Pallas kernels, fock_of(): pl.pallas_call(fock_kernel, out_shape=jax.ShapeDtypeStruct((owned, column...  29 us
    unnamed x20, local copies, waits for them, and re-layouts  9.45 us

profile of v1, /device:TPU:1, one launch (start us, length us, event | category | flops | bytes accessed | tf_op | source)
XLA Modules:
  0.0 136.4 jit_solution(18432059439804312058)
XLA Ops:
  0.6 0.8 copy.15
  1.4 0.0 copy-start
  1.4 1.9 %copy-done = bf16[1536,1024]{1,0:T(8,128)(2,1)S(1)} copy-done((bf16[1536,1024]{1,0:T(8,128)(2,1)S(1)}, bf16[1536,1024]{1,0:T(8,128)(2,1)}, u32[]{:S(2)}) %copy-start) | copy-done | bytes 3145752
  3.3 0.0 copy-start.1
  3.3 0.9 copy-done.1
  4.2 0.0 copy-start.2
  4.2 0.9 copy-done.2
  5.2 0.0 copy-start.3
  5.2 0.9 copy-done.3
  6.1 0.0 copy-start.4
  6.1 0.7 copy-done.4
  6.8 0.0 copy-start.5
  6.8 0.7 copy-done.5
  7.5 0.0 copy-start.6
  7.5 0.7 copy-done.6
  8.2 0.0 copy-start.7
  8.2 0.7 copy-done.7
  8.9 0.0 copy-start.8
  8.9 0.7 copy-done.8
  9.5 97.3 %exchange_of.1 = (f32[2,128]{1,0:T(2,128)S(1)}, f32[12,2,128]{2,1,0:T(2,128)S(1)}, bf16[3,8,128,1024]{3,2,1,0:T(8,128)(2,1)S(1)}, bf16[3,8,512,128]{3,2,1,0:T(8,128)(2,1)S(1)}, s32[3,8,128]{2,1,0:T(8,128)S(1)}) custom-call(bf16[12,128,1024]{2,1,0:T(8,128)(2,1)S(1)} %bitcast.10, bf16[2,128,512]{2,1,0:T(8,128)(2,1)S(1)} %copy-done.1, s32[8,128]{1,0:T(8,128)S(1)} %pad.4.names, ...), custom_call_target="tpu_custom_call" | custom-call | tf_op jit(solution)/shard_map/exchange_of/pallas_call | solution.py:508
  106.9 29.0 %fock_of.1 = f32[1536,1024]{1,0:T(8,128)} custom-call(s32[24,4]{1,0:T(8,128)S(1)} %subtract_bitcast_fusion.lists, bf16[3,8,512,128]{3,2,1,0:T(8,128)(2,1)S(1)} %get-tuple-element.8.basis_t, f32[24,128]{1,0:T(8,128)S(1)} %bitcast.11, bf16[3,8,128,1024]{3,2,1,0:T(8,128)(2,1)S(1)} %get-tuple-element.10.psi), custom_call_target="tpu_custom_call" | custom-call | tf_op jit(solution)/shard_map/fock_of/pallas_call | solution.py:599
  135.9 0.6 copy.20
  (2 shorter events, 0.0 us)
Async XLA Ops:
  1.4 1.9 %copy-start = (bf16[1536,1024]{1,0:T(8,128)(2,1)S(1)}, bf16[1536,1024]{1,0:T(8,128)(2,1)}, u32[]{:S(2)}) copy-start(bf16[1536,1024]{1,0:T(8,128)(2,1)} %param.12) | copy-start | bytes 9437188
  3.3 0.9 copy-start.1
  4.2 0.9 copy-start.2
  5.2 0.9 copy-start.3
  6.1 0.7 copy-start.4
  6.8 0.7 copy-start.5
  7.5 0.7 copy-start.6
  8.2 0.7 copy-start.7
  8.9 0.7 copy-start.8

commit v2 on v1

--- a/solution.py
+++ b/solution.py
@@ -57,13 +57,17 @@
 
 
 def exchange_kernel(
-    shape, layers, own, piece, names, atoms, weights, scale, shift, mw_in, aw_in, head,
-    pot, near, psi, basis_t, all_names,
-    rows, basis, lists, acc, part_out, part_in, relay, mw, aw, dens, dens_buf,
-    info, info_buf, rows_out, rows_buf, scaled_out, scaled_buf,
-    load, list_sem, name_sent, name_got, v_sent, v_got, z_sent, chip_sent,
-    part_sent, part_got, psi_sent, psi_got, passed, relay_sent, sent, got,
+    shape, layers, own, piece, names, *rest,
 ):
+    given, rest = rest[:7], rest[7:]
+    pot, near, psi, basis_t, all_names = rest[:5]
+    atoms, weights, scale, shift, mw, aw, head = rest[5:12]
+    (
+        rows, basis, lists, acc, part_out, part_in, relay, dens, dens_buf,
+        info, info_buf, rows_out, rows_buf, scaled_out, scaled_buf,
+        load, list_sem, name_sent, name_got, v_sent, v_got, z_sent, chip_sent,
+        part_sent, part_got, psi_sent, psi_got, passed, relay_sent, sent, got,
+    ) = rest[12:]
     n_grid, n_atom = shape
     n = n_grid * n_atom
     grid, atom = lax.axis_index("grid"), lax.axis_index("atom")
@@ -114,10 +118,13 @@
         far = jnp.where(reach == atom, t, n_atom - 1 - t)
         return jnp.where(t <= 2 * reach, close, far)
 
+    held_here = (
+        rows.at[pl.ds(1, owned)], basis.at[1, atom], all_names.at[1],
+        atoms, weights, scale, shift, mw, aw, head,
+    )
     loads = [
-        pltpu.make_async_copy(own, rows.at[pl.ds(1, owned)], load.at[0]),
-        pltpu.make_async_copy(mw_in, mw, load.at[1]),
-        pltpu.make_async_copy(aw_in, aw, load.at[2]),
+        pltpu.make_async_copy(source, target, load.at[i])
+        for i, (source, target) in enumerate(zip((own, piece, names, *given), held_here))
     ]
     for copy in loads:
         copy.start()
@@ -143,6 +150,8 @@
             piece, basis.at[1, atom], z_sent.at[0, 1, atom], v_got.at[1, atom], (grid, atom - 1)
         )
 
+    for copy in loads[1:5]:
+        copy.wait()
     total = float(ATOM_DEV * n_atom)
     named = atoms[...].astype(jnp.float32)
     lead = named[0:1, 0:1]
@@ -165,14 +174,12 @@
     to_all(info, info_buf, 1)
     info_buf[me] = info[...]
 
-    basis[1, atom] = piece[...]
-    all_names[1] = names[...]
     for edge in (0, owned + 1):
         rows[edge] = jnp.zeros((width, columns), rows.dtype)
 
     @pl.when(jnp.logical_not(has_outer))
     def _():
-        all_names[outer] = jnp.full_like(names, -1)
+        all_names[outer] = jnp.full(names.shape, -1, names.dtype)
         part_in[0] = jnp.zeros(part_in.shape[1:], part_in.dtype)
 
     @pl.when(has_outer)
@@ -189,7 +196,7 @@
     def product(slot, q, i, keep):
         chosen = []
         for j in range(picks):
-            block = lists[slot, q * nb + i, j] - first + 1
+            block = lists[slot, j, q * nb + i] - first + 1
             chosen.append(jnp.minimum(jnp.maximum(block, 0), owned + 1))
         values = basis[slot, q, i]
         for c in range(columns // tile):
@@ -269,41 +276,64 @@
                 1, q, i, psi.at[1, b], psi.at[inner, b], psi_sent.at[0], psi_got.at[inner, q]
             )
 
+    reach = jnp.minimum(atom, n_atom - 1 - atom)
+
+    def along(stream, slot, q):
+        for way in range(2):
+            able = (
+                jnp.logical_and(q <= atom, atom < n_atom - 1)
+                if way == 0
+                else jnp.logical_and(q >= atom, atom > 0)
+            )
+
+            @pl.when(able)
+            def _():
+                remote(
+                    basis.at[slot, q], basis.at[slot, q], z_sent.at[stream, way, q],
+                    v_got.at[slot, q], (grid, atom + 1 - 2 * way),
+                )
+
+    def spread_outer(t):
+        q = visit(t)
+
+        @pl.when(has_outer)
+        def _():
+            wait_bytes(basis.at[outer, q], v_got.at[outer, q])
+            along(1, outer, q)
+
+    def spread_own(t):
+        q = visit(t)
+        wait_bytes(basis.at[1, q], v_got.at[1, q])
+        along(0, 1, q)
+        remote(
+            basis.at[1, q], basis.at[outer, q], chip_sent.at[q], v_got.at[outer, q], (ig, atom)
+        )
+
+    spread_outer(0)
+
     @pl.loop(0, n_atom)
     def _(t):
         q = visit(t)
-
-        @pl.when(t > 0)
-        def _():
-            wait_bytes(piece, v_got.at[1, q])
-            remote(
-                basis.at[1, q], basis.at[outer, q], chip_sent.at[q], v_got.at[outer, q],
-                (ig, atom),
-            )
-
-        def along(stream, slot):
-            for way in range(2):
-                able = (
-                    jnp.logical_and(q <= atom, atom < n_atom - 1)
-                    if way == 0
-                    else jnp.logical_and(q >= atom, atom > 0)
-                )
-
-                @pl.when(able)
-                def _():
-                    remote(
-                        basis.at[slot, q], basis.at[slot, q], z_sent.at[stream, way, q],
-                        v_got.at[slot, q], (grid, atom + 1 - 2 * way),
-                    )
-
-        @pl.when(has_outer)
-        def _():
-            wait_bytes(piece, v_got.at[outer, q])
-            along(1, outer)
-
-        @pl.when(t > 0)
-        def _():
-            along(0, 1)
+        paired = jnp.logical_and(lax.rem(t, 2) == 1, t < 2 * reach)
+        fresh = jnp.logical_and(
+            t > 0, jnp.logical_or(lax.rem(t, 2) == 1, t > 2 * reach)
+        )
+
+        @pl.when(fresh)
+        def _():
+            spread_outer(t)
+
+        @pl.when(paired)
+        def _():
+            spread_outer(t + 1)
+
+        @pl.when(fresh)
+        def _():
+            spread_own(t)
+
+        @pl.when(paired)
+        def _():
+            spread_own(t + 1)
 
         @pl.when(has_outer)
         def _():
@@ -319,7 +349,7 @@
                     part_got.at[0, q],
                 )
 
-        wait_bytes(piece, v_got.at[inner, q])
+        wait_bytes(basis.at[inner, q], v_got.at[inner, q])
         for i in range(nb):
             b = q * nb + i
 
@@ -362,10 +392,6 @@
     rounds(0, psi_round)
     if n_atom >= 3:
         finish(visit(n_atom - 2))
-    forward(0, n_atom - 1)
-    finish(visit(n_atom - 1))
-    dens_buf[atom] = dens[atom]
-
     weight = to_columns(weights[...])[:, 0:1]
     spot = to_columns(place)
     hot = (spot == lax.broadcasted_iota(jnp.int32, spot.shape, 1).astype(jnp.float32)).astype(
@@ -375,8 +401,8 @@
     hot_t = jnp.concatenate([place[i : i + 1, :] == deep for i in range(nb)], axis=1).astype(
         jnp.bfloat16
     )
-    loads[1].wait()
-    loads[2].wait()
+    for copy in loads[5:]:
+        copy.wait()
     halves = scale.shape[1] // LANES
     wait_all(info_buf, got.at[1], n - 1)
     facts = info_buf[...].reshape(n * RUN, LANES)
@@ -391,6 +417,10 @@
             [same if k == h else none for k in range(halves)], axis=1
         ).reshape(n * RUN * halves, LANES)
         selects.append(jnp.transpose(full).astype(jnp.bfloat16))
+
+    forward(0, n_atom - 1)
+    finish(visit(n_atom - 1))
+    dens_buf[atom] = dens[atom]
 
     wait_all(dens_buf, got.at[0], n_atom - 1)
     density = to_columns(2.0 * jnp.sum(dens_buf[...], axis=0))
@@ -449,7 +479,7 @@
 
         @pl.when(q != atom)
         def _():
-            wait_bytes(piece, chip_sent.at[q])
+            wait_bytes(basis.at[1, q], chip_sent.at[q])
 
         for way in range(2):
             able = (
@@ -460,11 +490,11 @@
 
             @pl.when(able)
             def _():
-                wait_bytes(piece, z_sent.at[0, way, q])
+                wait_bytes(basis.at[1, q], z_sent.at[0, way, q])
 
             @pl.when(jnp.logical_and(able, has_outer))
             def _():
-                wait_bytes(piece, z_sent.at[1, way, q])
+                wait_bytes(basis.at[1, q], z_sent.at[1, way, q])
 
     @pl.when(has_outer)
     def _():
@@ -514,9 +544,12 @@
             jax.ShapeDtypeStruct((3, count, depth, points), bf16),
             jax.ShapeDtypeStruct((3, *names.shape), names.dtype),
         ),
-        in_specs=[HBM] + [VMEM] * 6 + [HBM, HBM, VMEM],
+        in_specs=[HBM] * 10,
         out_specs=(VMEM,) * 5,
         scratch_shapes=[
+            pltpu.VMEM(a.shape, a.dtype) for a in (atoms, weights, scale, shift, mw, aw, head)
+        ]
+        + [
             pltpu.VMEM((own.shape[0] + 2, width, columns), bf16),
             pltpu.VMEM((3, n_atom, nb, points, depth), bf16),
             pltpu.SMEM((3, *names.shape), names.dtype),
@@ -524,8 +557,6 @@
             pltpu.VMEM((2, count, points, columns), bf16),
             pltpu.VMEM((2, count, points, columns), bf16),
             pltpu.VMEM((2, n_atom, nb // 2, points, columns), bf16),
-            pltpu.VMEM(mw.shape, bf16),
-            pltpu.VMEM(aw.shape, bf16),
             pltpu.VMEM((n_atom, nb, points), f32),
             pltpu.VMEM((n_atom, nb, points), f32),
             pltpu.VMEM((RUN, LANES), f32),
@@ -534,7 +565,7 @@
             pltpu.VMEM((layers, n, packed, LANES), bf16),
             pltpu.VMEM((nb, points), f32),
             pltpu.VMEM((n, nb, points), f32),
-            dma((3,)),
+            dma((10,)),
             dma((1,)),
             dma((2,)),
             dma((3,)),
@@ -555,60 +586,112 @@
             collective_id=0, has_side_effects=True, vmem_limit_bytes=grant
         ),
         name="exchange_of",
-    )(own, piece, names, atoms, weights, scale, shift, mw, aw, head)
-
-
-def fock_kernel(lists, basis_t, near, psi, out, scaled):
-    step = pl.program_id(0)
+    )(
+        *(
+            pltpu.with_memory_space_constraint(a, pltpu.HBM)
+            for a in (own, piece, names, atoms, weights, scale, shift, mw, aw, head)
+        )
+    )
+
+
+QUAD = 4
+
+
+def fock_kernel(names, basis_t, near, psi, pot, out, pot_out, filled, table, held, done):
     groups, count, depth, points = basis_t.shape
-    picks = lists.shape[1]
-    width = depth // picks
-    wide = out.shape[1]
-    owned = out.shape[0] // width
-    columns = pl.ds(pl.multiple_of(step * wide, wide), wide)
-
-    out[...] = jnp.zeros_like(out)
-
-    @pl.loop(0, groups * count)
+    owned, width, columns = out.shape
+    picks = depth // width
+    most = groups * count
+    tile = min(columns, TILE)
+    first = lax.axis_index("grid") * owned
+    last = pltpu.make_async_copy(pot, pot_out, done.at[owned])
+    last.start()
+
+    @pl.loop(0, owned)
+    def _(r):
+        filled[r] = 0
+
+    @pl.loop(0, most)
     def _(s):
         k, b = s // count, lax.rem(s, count)
         for j in range(picks):
-            block = lists[s, j]
+            block = names[k, j, b] - first
 
             @pl.when(jnp.logical_and(block >= 0, block < owned))
             def _():
-                part = slice(j * width, (j + 1) * width)
-
-                @pl.when(step == 0)
+                n = filled[block]
+                table[block * most + n] = s * picks + j
+                filled[block] = n + 1
+
+    @pl.loop(0, owned)
+    def _(r):
+        n = filled[r]
+
+        @pl.when(n == 0)
+        def _():
+            held[r] = jnp.zeros((width, columns), jnp.float32)
+
+        @pl.loop(0, (n + QUAD - 1) // QUAD)
+        def _(m):
+            parts, values = [], []
+            for i in range(QUAD):
+                at = m * QUAD + i
+                entry = table[r * most + jnp.minimum(at, n - 1)]
+                s, j = entry // picks, lax.rem(entry, picks)
+                k, b = s // count, lax.rem(s, count)
+                taken = jnp.where(at < n, 1.0, 0.0)
+                part = basis_t[k, b, pl.ds(pl.multiple_of(j * width, width), width), :]
+                parts.append(
+                    (part.astype(jnp.float32) * (near[pl.ds(s, 1), :] * taken)).astype(
+                        jnp.bfloat16
+                    )
+                )
+                values.append((k, b))
+            left = jnp.concatenate(parts, axis=1)
+            for c in range(columns // tile):
+                at = pl.ds(c * tile, tile)
+                right = jnp.concatenate([psi[k, b, :, at] for k, b in values], axis=0)
+                value = jnp.dot(left, right, preferred_element_type=jnp.float32)
+
+                @pl.when(m == 0)
                 def _():
-                    scaled[s, part, :] = (
-                        basis_t[k, b, part, :].astype(jnp.float32) * near[pl.ds(s, 1), :]
-                    ).astype(jnp.bfloat16)
-
-                at = pl.ds(pl.multiple_of(block * width, width), width)
-                out[at, :] += jnp.dot(
-                    scaled[s, part, :], psi[k, b, :, columns], preferred_element_type=jnp.float32
-                )
-
-
-def fock_of(lists, basis_t, near, psi, owned):
+                    held[r, :, at] = value
+
+                @pl.when(m > 0)
+                def _():
+                    held[r, :, at] += value
+
+        pltpu.make_async_copy(held.at[r], out.at[r], done.at[r]).start()
+
+    for r in range(owned):
+        pltpu.make_async_copy(held.at[r], out.at[r], done.at[r]).wait()
+    last.wait()
+
+
+def fock_of(names, basis_t, near, psi, pot, owned):
     groups, count, depth, points = basis_t.shape
     columns = psi.shape[3]
-    wide = min(columns, 256)
-    grant = 2 * (9 * count * depth * points + 6 * count * points * wide + 4 * owned * wide)
+    width = depth // names.shape[1]
+    most = groups * count
     return pl.pallas_call(
         fock_kernel,
-        out_shape=jax.ShapeDtypeStruct((owned, columns), jnp.float32),
-        grid_spec=pltpu.PrefetchScalarGridSpec(
-            num_scalar_prefetch=1,
-            grid=(columns // wide,),
-            in_specs=[VMEM, VMEM, VMEM],
-            out_specs=pl.BlockSpec((owned, wide), lambda i, lists: (0, i)),
-            scratch_shapes=[pltpu.VMEM((groups * count, depth, points), jnp.bfloat16)],
+        out_shape=(
+            jax.ShapeDtypeStruct((owned, width, columns), jnp.float32),
+            jax.ShapeDtypeStruct(pot.shape, pot.dtype),
         ),
-        compiler_params=pltpu.CompilerParams(vmem_limit_bytes=grant + (12 << 20)),
+        in_specs=[pl.BlockSpec(memory_space=pltpu.SMEM), VMEM, VMEM, VMEM, VMEM],
+        out_specs=(HBM, HBM),
+        scratch_shapes=[
+            pltpu.SMEM((owned,), jnp.int32),
+            pltpu.SMEM((owned * most,), jnp.int32),
+            pltpu.VMEM((owned, width, columns), jnp.float32),
+            pltpu.SemaphoreType.DMA((owned + 1,)),
+        ],
+        compiler_params=pltpu.CompilerParams(
+            vmem_limit_bytes=4 * owned * width * columns + (8 << 20)
+        ),
         name="fock_of",
-    )(lists, basis_t, near, psi)
+    )(names, basis_t, near, psi, pot)
 
 
 def local(
@@ -628,13 +711,11 @@
     batches, points, depth = basis_values.shape
     picks = block_lists.shape[1]
     owned = own_rows // (depth // picks)
-    first = lax.axis_index("grid") * owned
-    names = jnp.pad(block_lists, ((0, 0), (0, LANES - picks)))
     potential, near, psi, basis_t, names = exchange_of(
         (n_grid, n_atom),
         orbitals.reshape(owned, own_rows // owned, -1),
         basis_values,
-        names,
+        block_lists.T,
         point_atoms.reshape(batches, points),
         point_weights.reshape(batches, points),
         embed_scale[None, :],
@@ -643,9 +724,8 @@
         atom_weight,
         head_weight[None, :],
     )
-    lists = names[:, :, :picks].reshape(-1, picks) - first
-    fock = fock_of(lists, basis_t, near.reshape(-1, points), psi, own_rows)
-    return (fock, potential.reshape(-1))
+    fock, potential = fock_of(names, basis_t, near.reshape(-1, points), psi, potential, owned)
+    return (fock.reshape(own_rows, -1), potential.reshape(-1))
 
 
 def solution(mesh):

time: 138 us -> 111 us (0.80)
  Pallas kernels: 126 us -> 108 us
  local copies, waits for them, and re-layouts: 9.46 us -> 0 us
    pallas_call x1, Pallas kernels: 29 us -> 13.6 us  [fock_of(): pl.pallas_call(fock_kernel, out_shape=(jax.ShapeDtypeStruct((owned, width...]
    unnamed x20 -> x0, local copies, waits for them, and re-layouts: 9.45 us -> none
    pallas_call x1, Pallas kernels: 97.3 us -> 94.6 us  [exchange_of(): pl.pallas_call(functools.partial(exchange_kernel, shape, layers), out_sha...]
where the time goes in v2:
time: 111 us; the launch traced here: 109 us
  Pallas kernels  108 us (97%)
    pallas_call x1, Pallas kernels, exchange_of(): pl.pallas_call(functools.partial(exchange_kernel, shape, layers), out_sha...  94.6 us
    pallas_call x1, Pallas kernels, fock_of(): pl.pallas_call(fock_kernel, out_shape=(jax.ShapeDtypeStruct((owned, width...  13.6 us

profile of v2, /device:TPU:1, one launch (start us, length us, event | category | flops | bytes accessed | tf_op | source)
XLA Modules:
  0.0 108.8 jit_solution(10214251054444182569)
XLA Ops:
  0.6 94.6 %exchange_of.1 = (f32[2,128]{1,0:T(2,128)S(1)}, f32[12,2,128]{2,1,0:T(2,128)S(1)}, bf16[3,8,128,1024]{3,2,1,0:T(8,128)(2,1)S(1)}, bf16[3,8,512,128]{3,2,1,0:T(8,128)(2,1)S(1)}, s32[3,4,8]{2,1,0:T(4,128)S(1)}) custom-call(bf16[12,128,1024]{2,1,0:T(8,128)(2,1)} %bitcast.11, bf16[2,128,512]{2,1,0:T(8,128)(2,1)} %piece.1, s32[4,8]{1,0:T(4,128)} %bitcast.12, ...), custom_call_target="tpu_custom_call" | custom-call | tf_op jit(solution)/shard_map/exchange_of/pallas_call | solution.py:538
  95.3 13.6 %fock_of.1 = (f32[12,128,1024]{2,1,0:T(8,128)}, f32[2,128]{1,0:T(2,128)}) custom-call(s32[3,4,8]{2,1,0:T(4,128)S(1)} %get-tuple-element.9.names, bf16[3,8,512,128]{3,2,1,0:T(8,128)(2,1)S(1)} %get-tuple-element.10.basis_t, f32[24,128]{1,0:T(8,128)S(1)} %bitcast.10, bf16[3,8,128,1024]{3,2,1,0:T(8,128)(2,1)S(1)} %get-tuple-element.12.psi, ...), custom_call_target="tpu_custom_call" | custom-call | tf_op jit(solution)/shard_map/fock_of/pallas_call | solution.py:676

commit v3 on v2

--- a/solution.py
+++ b/solution.py
@@ -64,7 +64,7 @@
     atoms, weights, scale, shift, mw, aw, head = rest[5:12]
     (
         rows, basis, lists, acc, part_out, part_in, relay, dens, dens_buf,
-        info, info_buf, rows_out, rows_buf, scaled_out, scaled_buf,
+        info, info_buf, rows_out, rows_buf, scaled_out,
         load, list_sem, name_sent, name_got, v_sent, v_got, z_sent, chip_sent,
         part_sent, part_got, psi_sent, psi_got, passed, relay_sent, sent, got,
     ) = rest[12:]
@@ -206,17 +206,14 @@
             )
             keep(at, jnp.dot(values, held, preferred_element_type=jnp.float32))
 
-    def outward(phase, q, i, source, target, sent_sem, got_sem):
-        @pl.when(whole)
-        def _():
-            remote(source, target, sent_sem, got_sem, (og, atom))
-
-        if i < direct:
-
-            @pl.when(at_split)
+    def outward(phase, q, i, source, target, sent_sem, got_sem, near_by=True, far=True):
+        if near_by:
+
+            @pl.when(whole if i >= direct else has_outer)
             def _():
                 remote(source, target, sent_sem, got_sem, (og, atom))
-        else:
+
+        if far and i >= direct:
 
             @pl.when(at_split)
             def _():
@@ -267,14 +264,19 @@
 
         at = pl.ds(q * nb, nb)
         remote(psi.at[1, at], psi.at[outer, at], psi_sent.at[1], psi_got.at[outer, q], (ig, atom))
-
-    def psi_round(r):
-        q = visit(r)
+        psi_outward(q, near_by=False)
+
+    def psi_outward(q, **which):
         for i in range(nb):
             b = q * nb + i
             outward(
-                1, q, i, psi.at[1, b], psi.at[inner, b], psi_sent.at[0], psi_got.at[inner, q]
+                1, q, i, psi.at[1, b], psi.at[inner, b], psi_sent.at[0], psi_got.at[inner, q],
+                **which,
             )
+
+    def psi_round(r):
+        psi_outward(visit(r), far=False)
+        forward(1, r)
 
     reach = jnp.minimum(atom, n_atom - 1 - atom)
 
@@ -309,6 +311,45 @@
             basis.at[1, q], basis.at[outer, q], chip_sent.at[q], v_got.at[outer, q], (ig, atom)
         )
 
+    def product_outer(q):
+        @pl.when(has_outer)
+        def _():
+            for i in range(nb):
+                b = q * nb + i
+
+                def keep(at, value):
+                    part_out[0, b, :, at] = value.astype(jnp.bfloat16)
+
+                product(outer, q, i, keep)
+                outward(
+                    0, q, i, part_out.at[0, b], part_in.at[0, b], part_sent.at[0],
+                    part_got.at[0, q],
+                )
+
+    def products_here(q):
+        wait_bytes(basis.at[inner, q], v_got.at[inner, q])
+        for i in range(nb):
+            b = q * nb + i
+
+            def keep(at, value):
+                part_out[1, b, :, at] = value.astype(jnp.bfloat16)
+
+            product(inner, q, i, keep)
+            remote(
+                part_out.at[1, b], part_in.at[1, b], part_sent.at[1], part_got.at[1, q],
+                (ig, atom),
+            )
+
+        for i in range(nb):
+            b = q * nb + i
+
+            def keep(at, value):
+                acc[b, :, at] = value
+
+            product(1, q, i, keep)
+            for slot in range(3):
+                basis_t[slot, b] = jnp.transpose(basis[slot, q, i])
+
     spread_outer(0)
 
     @pl.loop(0, n_atom)
@@ -327,6 +368,12 @@
         def _():
             spread_outer(t + 1)
 
+        product_outer(q)
+
+        @pl.when(t > 0)
+        def _():
+            products_here(visit(t - 1))
+
         @pl.when(fresh)
         def _():
             spread_own(t)
@@ -334,43 +381,6 @@
         @pl.when(paired)
         def _():
             spread_own(t + 1)
-
-        @pl.when(has_outer)
-        def _():
-            for i in range(nb):
-                b = q * nb + i
-
-                def keep(at, value):
-                    part_out[0, b, :, at] = value.astype(jnp.bfloat16)
-
-                product(outer, q, i, keep)
-                outward(
-                    0, q, i, part_out.at[0, b], part_in.at[0, b], part_sent.at[0],
-                    part_got.at[0, q],
-                )
-
-        wait_bytes(basis.at[inner, q], v_got.at[inner, q])
-        for i in range(nb):
-            b = q * nb + i
-
-            def keep(at, value):
-                part_out[1, b, :, at] = value.astype(jnp.bfloat16)
-
-            product(inner, q, i, keep)
-            remote(
-                part_out.at[1, b], part_in.at[1, b], part_sent.at[1], part_got.at[1, q],
-                (ig, atom),
-            )
-
-        for i in range(nb):
-            b = q * nb + i
-
-            def keep(at, value):
-                acc[b, :, at] = value
-
-            product(1, q, i, keep)
-            for slot in range(3):
-                basis_t[slot, b] = jnp.transpose(basis[slot, q, i])
 
         @pl.when(t >= 1)
         def _():
@@ -387,11 +397,9 @@
             if r * stops // n_atom == s:
                 act(r)
 
-    if n_atom < 3:
-        finish(visit(0))
     rounds(0, psi_round)
-    if n_atom >= 3:
-        finish(visit(n_atom - 2))
+    products_here(visit(n_atom - 1))
+    finish(visit(n_atom - 2))
     weight = to_columns(weights[...])[:, 0:1]
     spot = to_columns(place)
     hot = (spot == lax.broadcasted_iota(jnp.int32, spot.shape, 1).astype(jnp.float32)).astype(
@@ -440,7 +448,6 @@
         rounds(1 + layer, psi_round)
         rows_buf[layer, me] = rows_out[layer]
         wait_all(rows_buf.at[layer], got.at[2 + layer], n - 1)
-        rounds(layer, functools.partial(forward, 1))
         held = rows_buf[layer].reshape(n * RUN * halves, LANES)
         summed = jnp.concatenate(
             [jnp.dot(pick, held, preferred_element_type=jnp.float32) for pick in selects], axis=1
@@ -458,15 +465,39 @@
     pot[...] = to_rows(potential)
     final = 2 + layers
     scaled_out[...] = to_rows(weight * potential)
-    to_all(scaled_out, scaled_buf, final)
+
+    @pl.loop(1, n_atom)
+    def _(d):
+        remote(
+            scaled_out, near.at[n_atom + atom], sent.at[final], got.at[final],
+            (grid, lax.rem(atom + d, n_atom)),
+        )
+
+    @pl.when(has_outer)
+    def _():
+        @pl.loop(0, n_atom)
+        def _(d):
+            remote(
+                scaled_out, near.at[inner * n_atom + atom], sent.at[final + 1],
+                got.at[final + 1 + side], (og, d),
+            )
+
+    @pl.loop(0, n_atom)
+    def _(d):
+        remote(
+            scaled_out, near.at[outer * n_atom + atom], sent.at[final + 2],
+            got.at[final + 2 - side], (ig, d),
+        )
+
     rounds(layers + 1, psi_round)
-    scaled_buf[me] = scaled_out[...]
-    wait_all(scaled_buf, got.at[final], n - 1)
-    rounds(layers, functools.partial(forward, 1))
-    rounds(layers + 1, functools.partial(forward, 1))
-    for k in range(3):
-        group = jnp.clip(grid - 1 + k, 0, n_grid - 1)
-        near[k * n_atom : (k + 1) * n_atom] = scaled_buf[pl.ds(group * n_atom, n_atom)]
+    near[n_atom + atom] = scaled_out[...]
+    wait_all(near, got.at[final], n_atom - 1)
+
+    @pl.when(has_outer)
+    def _():
+        wait_all(near, got.at[final + 2 - side], n_atom)
+
+    wait_all(near, got.at[final + 1 + side], n_atom)
 
     @pl.loop(0, n_atom)
     def _(q):
@@ -517,7 +548,12 @@
     wait_all(info_buf, sent.at[1], n - 1)
     for layer in range(layers):
         wait_all(rows_buf.at[layer], sent.at[2 + layer], n - 1)
-    wait_all(scaled_buf, sent.at[final], n - 1)
+    wait_all(near, sent.at[final], n_atom - 1)
+    wait_all(near, sent.at[final + 2], n_atom)
+
+    @pl.when(has_outer)
+    def _():
+        wait_all(near, sent.at[final + 1], n_atom)
 
 
 def exchange_of(shape, own, piece, names, atoms, weights, scale, shift, mw, aw, head):
@@ -564,7 +600,6 @@
             pltpu.VMEM((layers, packed, LANES), bf16),
             pltpu.VMEM((layers, n, packed, LANES), bf16),
             pltpu.VMEM((nb, points), f32),
-            pltpu.VMEM((n, nb, points), f32),
             dma((10,)),
             dma((1,)),
             dma((2,)),
@@ -579,8 +614,8 @@
             dma((3, n_atom)),
             dma((2, n_atom)),
             dma((2,)),
-            dma((3 + layers,)),
-            dma((3 + layers,)),
+            dma((5 + layers,)),
+            dma((5 + layers,)),
         ],
         compiler_params=pltpu.CompilerParams(
             collective_id=0, has_side_effects=True, vmem_limit_bytes=grant

time: 111 us -> 105 us (0.946); the launches traced: 109 us -> 105 us
  Pallas kernels: 108 us -> 104 us
    pallas_call x1, Pallas kernels: 94.6 us -> 88.8 us  [exchange_of(): pl.pallas_call(functools.partial(exchange_kernel, shape, layers), out_sha...]
    pallas_call x1, Pallas kernels: 13.6 us -> 15.4 us  [fock_of(): pl.pallas_call(fock_kernel, out_shape=(jax.ShapeDtypeStruct((owned, width...]
where the time goes in v3:
time: 105 us
  Pallas kernels  104 us (99%)
    pallas_call x1, Pallas kernels, exchange_of(): pl.pallas_call(functools.partial(exchange_kernel, shape, layers), out_sha...  88.8 us
    pallas_call x1, Pallas kernels, fock_of(): pl.pallas_call(fock_kernel, out_shape=(jax.ShapeDtypeStruct((owned, width...  15.4 us

profile of v3, /device:TPU:1, one launch (start us, length us, event | category | flops | bytes accessed | tf_op | source)
XLA Modules:
  0.0 104.8 jit_solution(17668983537762640908)
XLA Ops:
  0.6 88.8 %exchange_of.1 = (f32[2,128]{1,0:T(2,128)S(1)}, f32[12,2,128]{2,1,0:T(2,128)S(1)}, bf16[3,8,128,1024]{3,2,1,0:T(8,128)(2,1)S(1)}, bf16[3,8,512,128]{3,2,1,0:T(8,128)(2,1)S(1)}, s32[3,4,8]{2,1,0:T(4,128)S(1)}) custom-call(bf16[12,128,1024]{2,1,0:T(8,128)(2,1)} %bitcast.11, bf16[2,128,512]{2,1,0:T(8,128)(2,1)} %piece.1, s32[4,8]{1,0:T(4,128)} %bitcast.12, ...), custom_call_target="tpu_custom_call" | custom-call | tf_op jit(solution)/shard_map/exchange_of/pallas_call | solution.py:574
  89.4 15.4 %fock_of.1 = (f32[12,128,1024]{2,1,0:T(8,128)}, f32[2,128]{1,0:T(2,128)}) custom-call(s32[3,4,8]{2,1,0:T(4,128)S(1)} %get-tuple-element.9.names, bf16[3,8,512,128]{3,2,1,0:T(8,128)(2,1)S(1)} %get-tuple-element.10.basis_t, f32[24,128]{1,0:T(8,128)S(1)} %bitcast.10, bf16[3,8,128,1024]{3,2,1,0:T(8,128)(2,1)S(1)} %get-tuple-element.12.psi, ...), custom_call_target="tpu_custom_call" | custom-call | tf_op jit(solution)/shard_map/fock_of/pallas_call | solution.py:711

commit v4 on v3

--- a/solution.py
+++ b/solution.py
@@ -636,31 +636,29 @@
     groups, count, depth, points = basis_t.shape
     owned, width, columns = out.shape
     picks = depth // width
-    most = groups * count
+    most = groups * count * picks
     tile = min(columns, TILE)
     first = lax.axis_index("grid") * owned
     last = pltpu.make_async_copy(pot, pot_out, done.at[owned])
     last.start()
 
+    @pl.loop(0, owned + 2)
+    def _(r):
+        filled[r] = 0
+
+    for k in range(groups):
+
+        @pl.loop(0, count)
+        def _(b):
+            for j in range(picks):
+                row = jnp.minimum(jnp.maximum(names[k, j, b] - first + 1, 0), owned + 1)
+                n = filled[row]
+                table[row * most + n] = (k * count + b) * picks + j
+                filled[row] = n + 1
+
     @pl.loop(0, owned)
     def _(r):
-        filled[r] = 0
-
-    @pl.loop(0, most)
-    def _(s):
-        k, b = s // count, lax.rem(s, count)
-        for j in range(picks):
-            block = names[k, j, b] - first
-
-            @pl.when(jnp.logical_and(block >= 0, block < owned))
-            def _():
-                n = filled[block]
-                table[block * most + n] = s * picks + j
-                filled[block] = n + 1
-
-    @pl.loop(0, owned)
-    def _(r):
-        n = filled[r]
+        n = filled[r + 1]
 
         @pl.when(n == 0)
         def _():
@@ -671,7 +669,7 @@
             parts, values = [], []
             for i in range(QUAD):
                 at = m * QUAD + i
-                entry = table[r * most + jnp.minimum(at, n - 1)]
+                entry = table[(r + 1) * most + jnp.minimum(at, n - 1)]
                 s, j = entry // picks, lax.rem(entry, picks)
                 k, b = s // count, lax.rem(s, count)
                 taken = jnp.where(at < n, 1.0, 0.0)
@@ -683,18 +681,24 @@
                 )
                 values.append((k, b))
             left = jnp.concatenate(parts, axis=1)
-            for c in range(columns // tile):
-                at = pl.ds(c * tile, tile)
-                right = jnp.concatenate([psi[k, b, :, at] for k, b in values], axis=0)
-                value = jnp.dot(left, right, preferred_element_type=jnp.float32)
-
-                @pl.when(m == 0)
-                def _():
-                    held[r, :, at] = value
-
-                @pl.when(m > 0)
-                def _():
-                    held[r, :, at] += value
+
+            def multiply(first_time):
+                for c in range(columns // tile):
+                    at = pl.ds(c * tile, tile)
+                    right = jnp.concatenate([psi[k, b, :, at] for k, b in values], axis=0)
+                    value = jnp.dot(left, right, preferred_element_type=jnp.float32)
+                    if first_time:
+                        held[r, :, at] = value
+                    else:
+                        held[r, :, at] += value
+
+            @pl.when(m == 0)
+            def _():
+                multiply(True)
+
+            @pl.when(m > 0)
+            def _():
+                multiply(False)
 
         pltpu.make_async_copy(held.at[r], out.at[r], done.at[r]).start()
 
@@ -707,7 +711,7 @@
     groups, count, depth, points = basis_t.shape
     columns = psi.shape[3]
     width = depth // names.shape[1]
-    most = groups * count
+    most = groups * depth // width * count
     return pl.pallas_call(
         fock_kernel,
         out_shape=(
@@ -717,8 +721,8 @@
         in_specs=[pl.BlockSpec(memory_space=pltpu.SMEM), VMEM, VMEM, VMEM, VMEM],
         out_specs=(HBM, HBM),
         scratch_shapes=[
-            pltpu.SMEM((owned,), jnp.int32),
-            pltpu.SMEM((owned * most,), jnp.int32),
+            pltpu.SMEM((owned + 2,), jnp.int32),
+            pltpu.SMEM(((owned + 2) * most,), jnp.int32),
             pltpu.VMEM((owned, width, columns), jnp.float32),
             pltpu.SemaphoreType.DMA((owned + 1,)),
         ],

time: 105 us -> 97.9 us (0.932)
  Pallas kernels: 104 us -> 97.3 us
    pallas_call x1, Pallas kernels: 15.4 us -> 8.56 us  [fock_of(): pl.pallas_call(fock_kernel, out_shape=(jax.ShapeDtypeStruct((owned, width...]
where the time goes in v4:
time: 97.9 us; the launch traced here: 98 us
  Pallas kernels  97.3 us (99%)
    pallas_call x1, Pallas kernels, exchange_of(): pl.pallas_call(functools.partial(exchange_kernel, shape, layers), out_sha...  88.8 us
    pallas_call x1, Pallas kernels, fock_of(): pl.pallas_call(fock_kernel, out_shape=(jax.ShapeDtypeStruct((owned, width...  8.56 us

profile of v4, /device:TPU:1, one launch (start us, length us, event | category | flops | bytes accessed | tf_op | source)
XLA Modules:
  0.0 98.0 jit_solution(212902475142510691)
XLA Ops:
  0.6 88.8 %exchange_of.1 = (f32[2,128]{1,0:T(2,128)S(1)}, f32[12,2,128]{2,1,0:T(2,128)S(1)}, bf16[3,8,128,1024]{3,2,1,0:T(8,128)(2,1)S(1)}, bf16[3,8,512,128]{3,2,1,0:T(8,128)(2,1)S(1)}, s32[3,4,8]{2,1,0:T(4,128)S(1)}) custom-call(bf16[12,128,1024]{2,1,0:T(8,128)(2,1)} %bitcast.11, bf16[2,128,512]{2,1,0:T(8,128)(2,1)} %piece.1, s32[4,8]{1,0:T(4,128)} %bitcast.12, ...), custom_call_target="tpu_custom_call" | custom-call | tf_op jit(solution)/shard_map/exchange_of/pallas_call | solution.py:574
  89.4 8.6 %fock_of.1 = (f32[12,128,1024]{2,1,0:T(8,128)}, f32[2,128]{1,0:T(2,128)}) custom-call(s32[3,4,8]{2,1,0:T(4,128)S(1)} %get-tuple-element.9.names, bf16[3,8,512,128]{3,2,1,0:T(8,128)(2,1)S(1)} %get-tuple-element.10.basis_t, f32[24,128]{1,0:T(8,128)S(1)} %bitcast.10, bf16[3,8,128,1024]{3,2,1,0:T(8,128)(2,1)S(1)} %get-tuple-element.12.psi, ...), custom_call_target="tpu_custom_call" | custom-call | tf_op jit(solution)/shard_map/fock_of/pallas_call | solution.py:715

commit v5 on v4

--- a/solution.py
+++ b/solution.py
@@ -67,11 +67,11 @@
         info, info_buf, rows_out, rows_buf, scaled_out,
         load, list_sem, name_sent, name_got, v_sent, v_got, z_sent, chip_sent,
         part_sent, part_got, psi_sent, psi_got, passed, relay_sent, sent, got,
+        relay_v, v_passed, pair_sent, pair_got,
     ) = rest[12:]
     n_grid, n_atom = shape
     n = n_grid * n_atom
     grid, atom = lax.axis_index("grid"), lax.axis_index("atom")
-    me = grid * n_atom + atom
     last, middle = n_grid - 1, n_grid // 2
     side = lax.rem(grid, 2)
     outer, inner = 2 * side, 2 - 2 * side
@@ -100,14 +100,24 @@
             device_id_type=MESH,
         ).start()
 
-    def to_all(source, held, k):
-        @pl.loop(1, n)
+    half = n // 2
+    place_here = (grid // 2) * n_atom + atom
+    slot_here = side * half + place_here
+
+    def to_chips(source, held, k):
+        @pl.loop(1, half)
         def _(d):
-            t = lax.rem(me + d, n)
+            t = lax.rem(place_here + d, half)
             remote(
-                source, held.at[me], sent.at[k], got.at[k],
-                (t // n_atom, lax.rem(t, n_atom)),
-            )
+                source, held.at[slot_here], sent.at[k], got.at[k],
+                ((t // n_atom) * 2 + side, lax.rem(t, n_atom)),
+            )
+
+    def hand_over(held, k):
+        wait_bytes(held.at[pl.ds(0, half - 1)], got.at[k])
+        slab = held.at[pl.ds(side * half, half)]
+        remote(slab, slab, pair_sent.at[k], pair_got.at[k], (ig, atom))
+        wait_bytes(held.at[pl.ds(0, half)], pair_got.at[k])
 
     def wait_all(held, sem, count):
         wait_bytes(held.at[pl.ds(0, count)], sem)
@@ -133,7 +143,22 @@
     @pl.when(has_outer)
     def _():
         remote(names, all_names.at[inner], name_sent.at[0], name_got.at[inner], (og, atom))
+
+    @pl.when(whole if relayed else has_outer)
+    def _():
         remote(piece, basis.at[inner, atom], v_sent.at[0], v_got.at[inner, atom], (og, atom))
+
+    if relayed:
+
+        @pl.when(at_split)
+        def _():
+            part = pl.ds(direct, relayed)
+            remote(piece.at[part], relay_v, v_sent.at[0], v_passed.at[0], (relay_to, atom))
+            part = pl.ds(0, direct)
+            remote(
+                piece.at[part], basis.at[inner, atom, part], v_sent.at[0],
+                v_got.at[inner, atom], (og, atom),
+            )
 
     remote(names, all_names.at[outer], name_sent.at[1], name_got.at[outer], (ig, atom))
     remote(piece, basis.at[outer, atom], v_sent.at[1], v_got.at[outer, atom], (ig, atom))
@@ -171,8 +196,19 @@
         wrapped(start + run, total),
         mass,
     )
-    to_all(info, info_buf, 1)
-    info_buf[me] = info[...]
+    to_chips(info, info_buf, 1)
+    info_buf[slot_here] = info[...]
+
+    if relayed:
+
+        @pl.when(relays)
+        def _():
+            wait_bytes(relay_v, v_passed.at[0])
+            remote(
+                relay_v, basis.at[inner, atom, pl.ds(direct, relayed)], v_passed.at[1],
+                v_got.at[inner, atom], (forward_to, atom),
+            )
+
 
     for edge in (0, owned + 1):
         rows[edge] = jnp.zeros((width, columns), rows.dtype)
@@ -412,7 +448,7 @@
     for copy in loads[5:]:
         copy.wait()
     halves = scale.shape[1] // LANES
-    wait_all(info_buf, got.at[1], n - 1)
+    hand_over(info_buf, 1)
     facts = info_buf[...].reshape(n * RUN, LANES)
     same = (facts[:, 0:1] == mine).astype(jnp.float32)
     mass = jnp.sum(same * facts[:, LANES // 2 : LANES // 2 + 1], axis=0, keepdims=True)
@@ -444,10 +480,10 @@
         rows_out[layer] = jnp.concatenate(
             [part[0:RUN, h * LANES : (h + 1) * LANES] for h in range(halves)], axis=0
         ).astype(jnp.bfloat16)
-        to_all(rows_out.at[layer], rows_buf.at[layer], 2 + layer)
+        to_chips(rows_out.at[layer], rows_buf.at[layer], 2 + layer)
+        rows_buf[layer, slot_here] = rows_out[layer]
         rounds(1 + layer, psi_round)
-        rows_buf[layer, me] = rows_out[layer]
-        wait_all(rows_buf.at[layer], got.at[2 + layer], n - 1)
+        hand_over(rows_buf.at[layer], 2 + layer)
         held = rows_buf[layer].reshape(n * RUN * halves, LANES)
         summed = jnp.concatenate(
             [jnp.dot(pick, held, preferred_element_type=jnp.float32) for pick in selects], axis=1
@@ -541,13 +577,14 @@
 
     @pl.when(relays)
     def _():
+        wait_bytes(relay_v, v_passed.at[1])
         for phase in range(2):
             wait_bytes(relay.at[phase], relay_sent.at[phase])
 
     wait_all(dens_buf, sent.at[0], n_atom - 1)
-    wait_all(info_buf, sent.at[1], n - 1)
-    for layer in range(layers):
-        wait_all(rows_buf.at[layer], sent.at[2 + layer], n - 1)
+    for k, held in enumerate([info_buf] + [rows_buf.at[layer] for layer in range(layers)]):
+        wait_all(held, sent.at[1 + k], half - 1)
+        wait_all(held, pair_sent.at[1 + k], half)
     wait_all(near, sent.at[final], n_atom - 1)
     wait_all(near, sent.at[final + 2], n_atom)
 
@@ -616,6 +653,10 @@
             dma((2,)),
             dma((5 + layers,)),
             dma((5 + layers,)),
+            pltpu.VMEM((max(nb // 2, 1), points, depth), bf16),
+            dma((2,)),
+            dma((2 + layers,)),
+            dma((2 + layers,)),
         ],
         compiler_params=pltpu.CompilerParams(
             collective_id=0, has_side_effects=True, vmem_limit_bytes=grant

time: 97.9 us -> 94.1 us (0.961)
  Pallas kernels: 97.3 us -> 94 us
    pallas_call x1, Pallas kernels: 88.8 us -> 86.2 us  [exchange_of(): pl.pallas_call(functools.partial(exchange_kernel, shape, layers), out_sha...]
where the time goes in v5:
time: 94.1 us; the launch traced here: 94.6 us
  Pallas kernels  94 us (100%)
    pallas_call x1, Pallas kernels, exchange_of(): pl.pallas_call(functools.partial(exchange_kernel, shape, layers), out_sha...  86.2 us
    pallas_call x1, Pallas kernels, fock_of(): pl.pallas_call(fock_kernel, out_shape=(jax.ShapeDtypeStruct((owned, width...  7.83 us

profile of v5, /device:TPU:1, one launch (start us, length us, event | category | flops | bytes accessed | tf_op | source)
XLA Modules:
  0.0 94.6 jit_solution(4999325201309445767)
XLA Ops:
  0.6 86.2 %exchange_of.1 = (f32[2,128]{1,0:T(2,128)S(1)}, f32[12,2,128]{2,1,0:T(2,128)S(1)}, bf16[3,8,128,1024]{3,2,1,0:T(8,128)(2,1)S(1)}, bf16[3,8,512,128]{3,2,1,0:T(8,128)(2,1)S(1)}, s32[3,4,8]{2,1,0:T(4,128)S(1)}) custom-call(bf16[12,128,1024]{2,1,0:T(8,128)(2,1)} %bitcast.11, bf16[2,128,512]{2,1,0:T(8,128)(2,1)} %piece.1, s32[4,8]{1,0:T(4,128)} %bitcast.12, ...), custom_call_target="tpu_custom_call" | custom-call | tf_op jit(solution)/shard_map/exchange_of/pallas_call | solution.py:611
  86.8 7.8 %fock_of.1 = (f32[12,128,1024]{2,1,0:T(8,128)}, f32[2,128]{1,0:T(2,128)}) custom-call(s32[3,4,8]{2,1,0:T(4,128)S(1)} %get-tuple-element.9.names, bf16[3,8,512,128]{3,2,1,0:T(8,128)(2,1)S(1)} %get-tuple-element.10.basis_t, f32[24,128]{1,0:T(8,128)S(1)} %bitcast.10, bf16[3,8,128,1024]{3,2,1,0:T(8,128)(2,1)S(1)} %get-tuple-element.12.psi, ...), custom_call_target="tpu_custom_call" | custom-call | tf_op jit(solution)/shard_map/fock_of/pallas_call | solution.py:756

commit v6 on v5

--- a/solution.py
+++ b/solution.py
@@ -13,6 +13,7 @@
 HBM = pl.BlockSpec(memory_space=pltpu.HBM)
 MESH = pl.DeviceIdType.MESH
 TILE = 256
+PARTS = (2, 2, 2, 2)
 
 
 def wait_bytes(ref, sem):
@@ -67,7 +68,7 @@
         info, info_buf, rows_out, rows_buf, scaled_out,
         load, list_sem, name_sent, name_got, v_sent, v_got, z_sent, chip_sent,
         part_sent, part_got, psi_sent, psi_got, passed, relay_sent, sent, got,
-        relay_v, v_passed, pair_sent, pair_got,
+        relay_v, v_passed, pair_sent, pair_got, v_first,
     ) = rest[12:]
     n_grid, n_atom = shape
     n = n_grid * n_atom
@@ -144,21 +145,21 @@
     def _():
         remote(names, all_names.at[inner], name_sent.at[0], name_got.at[inner], (og, atom))
 
-    @pl.when(whole if relayed else has_outer)
-    def _():
-        remote(piece, basis.at[inner, atom], v_sent.at[0], v_got.at[inner, atom], (og, atom))
-
-    if relayed:
-
-        @pl.when(at_split)
-        def _():
-            part = pl.ds(direct, relayed)
-            remote(piece.at[part], relay_v, v_sent.at[0], v_passed.at[0], (relay_to, atom))
-            part = pl.ds(0, direct)
-            remote(
-                piece.at[part], basis.at[inner, atom, part], v_sent.at[0],
-                v_got.at[inner, atom], (og, atom),
-            )
+    for i in range(nb):
+        target = basis.at[inner, atom, i]
+
+        @pl.when(has_outer if i < direct else whole)
+        def _():
+            remote(piece.at[i], target, v_sent.at[0], v_first.at[i], (og, atom))
+
+        if i >= direct:
+
+            @pl.when(at_split)
+            def _():
+                remote(
+                    piece.at[i], relay_v.at[i - direct], v_sent.at[0], v_passed.at[0],
+                    (relay_to, atom),
+                )
 
     remote(names, all_names.at[outer], name_sent.at[1], name_got.at[outer], (ig, atom))
     remote(piece, basis.at[outer, atom], v_sent.at[1], v_got.at[outer, atom], (ig, atom))
@@ -204,11 +205,11 @@
         @pl.when(relays)
         def _():
             wait_bytes(relay_v, v_passed.at[0])
-            remote(
-                relay_v, basis.at[inner, atom, pl.ds(direct, relayed)], v_passed.at[1],
-                v_got.at[inner, atom], (forward_to, atom),
-            )
-
+            for i in range(direct, nb):
+                remote(
+                    relay_v.at[i - direct], basis.at[inner, atom, i], v_passed.at[1],
+                    v_first.at[i], (forward_to, atom),
+                )
 
     for edge in (0, owned + 1):
         rows[edge] = jnp.zeros((width, columns), rows.dtype)
@@ -272,7 +273,8 @@
                 target, got_sem = psi.at[inner, at], psi_got.at[inner, q]
             remote(held, target, relay_sent.at[phase], got_sem, (forward_to, atom))
 
-    def finish(q):
+    def finish(t):
+        q = visit(t)
         wait_bytes(part_in.at[1, pl.ds(q * nb, nb)], part_got.at[1, q])
 
         @pl.when(has_outer)
@@ -300,19 +302,21 @@
 
         at = pl.ds(q * nb, nb)
         remote(psi.at[1, at], psi.at[outer, at], psi_sent.at[1], psi_got.at[outer, q], (ig, atom))
-        psi_outward(q, near_by=False)
-
-    def psi_outward(q, **which):
         for i in range(nb):
-            b = q * nb + i
-            outward(
-                1, q, i, psi.at[1, b], psi.at[inner, b], psi_sent.at[0], psi_got.at[inner, q],
-                **which,
-            )
-
-    def psi_round(r):
-        psi_outward(visit(r), far=False)
-        forward(1, r)
+            psi_outward(t, i, near_by=False)
+
+    def psi_outward(r, i, **which):
+        q = visit(r)
+        b = q * nb + i
+        outward(
+            1, q, i, psi.at[1, b], psi.at[inner, b], psi_sent.at[0], psi_got.at[inner, q],
+            **which,
+        )
+
+    def psi_unit(r, i):
+        psi_outward(r, i, far=False)
+        if i == nb - 1:
+            forward(1, r)
 
     reach = jnp.minimum(atom, n_atom - 1 - atom)
 
@@ -339,6 +343,21 @@
             wait_bytes(basis.at[outer, q], v_got.at[outer, q])
             along(1, outer, q)
 
+    def send_first():
+        for i in range(nb):
+            mine_first = basis.at[outer, atom, i]
+            wait_bytes(mine_first, v_first.at[i])
+            for way in range(2):
+
+                @pl.when(atom < n_atom - 1 if way == 0 else atom > 0)
+                def _():
+                    remote(
+                        mine_first, mine_first, z_sent.at[1, way, atom], v_got.at[outer, atom],
+                        (grid, atom + 1 - 2 * way),
+                    )
+
+            outer_part(atom, i)
+
     def spread_own(t):
         q = visit(t)
         wait_bytes(basis.at[1, q], v_got.at[1, q])
@@ -347,20 +366,20 @@
             basis.at[1, q], basis.at[outer, q], chip_sent.at[q], v_got.at[outer, q], (ig, atom)
         )
 
+    def outer_part(q, i):
+        b = q * nb + i
+
+        def keep(at, value):
+            part_out[0, b, :, at] = value.astype(jnp.bfloat16)
+
+        product(outer, q, i, keep)
+        outward(
+            0, q, i, part_out.at[0, b], part_in.at[0, b], part_sent.at[0], part_got.at[0, q]
+        )
+
     def product_outer(q):
-        @pl.when(has_outer)
-        def _():
-            for i in range(nb):
-                b = q * nb + i
-
-                def keep(at, value):
-                    part_out[0, b, :, at] = value.astype(jnp.bfloat16)
-
-                product(outer, q, i, keep)
-                outward(
-                    0, q, i, part_out.at[0, b], part_in.at[0, b], part_sent.at[0],
-                    part_got.at[0, q],
-                )
+        for i in range(nb):
+            outer_part(q, i)
 
     def products_here(q):
         wait_bytes(basis.at[inner, q], v_got.at[inner, q])
@@ -386,7 +405,9 @@
             for slot in range(3):
                 basis_t[slot, b] = jnp.transpose(basis[slot, q, i])
 
-    spread_outer(0)
+    @pl.when(has_outer)
+    def _():
+        send_first()
 
     @pl.loop(0, n_atom)
     def _(t):
@@ -404,7 +425,9 @@
         def _():
             spread_outer(t + 1)
 
-        product_outer(q)
+        @pl.when(jnp.logical_and(t > 0, has_outer))
+        def _():
+            product_outer(q)
 
         @pl.when(t > 0)
         def _():
@@ -424,18 +447,18 @@
 
         @pl.when(t >= 2)
         def _():
-            finish(visit(t - 2))
-
-    stops = layers + 2
-
-    def rounds(s, act):
-        for r in range(n_atom):
-            if r * stops // n_atom == s:
-                act(r)
-
-    rounds(0, psi_round)
+            finish(t - 2)
+
+    ends = [sum(PARTS[: s + 1]) for s in range(len(PARTS))]
+
+    def send_psi(s):
+        for u in range(n_atom * nb):
+            if sum(u * ends[-1] >= end * n_atom * nb for end in ends) == s:
+                psi_unit(u // nb, u % nb)
+
+    send_psi(0)
     products_here(visit(n_atom - 1))
-    finish(visit(n_atom - 2))
+    finish(n_atom - 2)
     weight = to_columns(weights[...])[:, 0:1]
     spot = to_columns(place)
     hot = (spot == lax.broadcasted_iota(jnp.int32, spot.shape, 1).astype(jnp.float32)).astype(
@@ -463,7 +486,7 @@
         selects.append(jnp.transpose(full).astype(jnp.bfloat16))
 
     forward(0, n_atom - 1)
-    finish(visit(n_atom - 1))
+    finish(n_atom - 1)
     dens_buf[atom] = dens[atom]
 
     wait_all(dens_buf, got.at[0], n_atom - 1)
@@ -482,7 +505,7 @@
         ).astype(jnp.bfloat16)
         to_chips(rows_out.at[layer], rows_buf.at[layer], 2 + layer)
         rows_buf[layer, slot_here] = rows_out[layer]
-        rounds(1 + layer, psi_round)
+        send_psi(1 + layer)
         hand_over(rows_buf.at[layer], 2 + layer)
         held = rows_buf[layer].reshape(n * RUN * halves, LANES)
         summed = jnp.concatenate(
@@ -525,7 +548,7 @@
             got.at[final + 2 - side], (ig, d),
         )
 
-    rounds(layers + 1, psi_round)
+    send_psi(layers + 1)
     near[n_atom + atom] = scaled_out[...]
     wait_all(near, got.at[final], n_atom - 1)
 
@@ -657,6 +680,7 @@
             dma((2,)),
             dma((2 + layers,)),
             dma((2 + layers,)),
+            dma((nb,)),
         ],
         compiler_params=pltpu.CompilerParams(
             collective_id=0, has_side_effects=True, vmem_limit_bytes=grant
@@ -670,7 +694,7 @@
     )
 
 
-QUAD = 4
+MANY = 6
 
 
 def fock_kernel(names, basis_t, near, psi, pot, out, pot_out, filled, table, held, done):
@@ -705,41 +729,36 @@
         def _():
             held[r] = jnp.zeros((width, columns), jnp.float32)
 
-        @pl.loop(0, (n + QUAD - 1) // QUAD)
-        def _(m):
+        def multiply(begin, many, first_time):
             parts, values = [], []
-            for i in range(QUAD):
-                at = m * QUAD + i
-                entry = table[(r + 1) * most + jnp.minimum(at, n - 1)]
+            for i in range(many):
+                entry = table[(r + 1) * most + begin + i]
                 s, j = entry // picks, lax.rem(entry, picks)
                 k, b = s // count, lax.rem(s, count)
-                taken = jnp.where(at < n, 1.0, 0.0)
                 part = basis_t[k, b, pl.ds(pl.multiple_of(j * width, width), width), :]
                 parts.append(
-                    (part.astype(jnp.float32) * (near[pl.ds(s, 1), :] * taken)).astype(
-                        jnp.bfloat16
-                    )
+                    (part.astype(jnp.float32) * near[pl.ds(s, 1), :]).astype(jnp.bfloat16)
                 )
                 values.append((k, b))
             left = jnp.concatenate(parts, axis=1)
-
-            def multiply(first_time):
-                for c in range(columns // tile):
-                    at = pl.ds(c * tile, tile)
-                    right = jnp.concatenate([psi[k, b, :, at] for k, b in values], axis=0)
-                    value = jnp.dot(left, right, preferred_element_type=jnp.float32)
-                    if first_time:
-                        held[r, :, at] = value
-                    else:
-                        held[r, :, at] += value
-
-            @pl.when(m == 0)
+            for c in range(columns // tile):
+                at = pl.ds(c * tile, tile)
+                right = jnp.concatenate([psi[k, b, :, at] for k, b in values], axis=0)
+                value = jnp.dot(left, right, preferred_element_type=jnp.float32)
+                if first_time:
+                    held[r, :, at] = value
+                else:
+                    held[r, :, at] += value
+
+        for many in range(1, MANY + 1):
+
+            @pl.when(n == many if many < MANY else n >= many)
             def _():
-                multiply(True)
-
-            @pl.when(m > 0)
-            def _():
-                multiply(False)
+                multiply(0, many, True)
+
+        @pl.loop(MANY, jnp.maximum(n, MANY))
+        def _(m):
+            multiply(m, 1, False)
 
         pltpu.make_async_copy(held.at[r], out.at[r], done.at[r]).start()
 

time: 94.1 us -> 92.6 us (0.984)
  Pallas kernels: 94 us -> 91.8 us
    pallas_call x1, Pallas kernels: 7.83 us -> 6.44 us  [fock_of(): pl.pallas_call(fock_kernel, out_shape=(jax.ShapeDtypeStruct((owned, width...]
where the time goes in v6:
time: 92.6 us; the launch traced here: 92.5 us
  Pallas kernels  91.8 us (99%)
    pallas_call x1, Pallas kernels, exchange_of(): pl.pallas_call(functools.partial(exchange_kernel, shape, layers), out_sha...  85.4 us
    pallas_call x1, Pallas kernels, fock_of(): pl.pallas_call(fock_kernel, out_shape=(jax.ShapeDtypeStruct((owned, width...  6.44 us

profile of v6, /device:TPU:1, one launch (start us, length us, event | category | flops | bytes accessed | tf_op | source)
XLA Modules:
  0.0 92.5 jit_solution(160489558957583533)
XLA Ops:
  0.6 85.4 %exchange_of.1 = (f32[2,128]{1,0:T(2,128)S(1)}, f32[12,2,128]{2,1,0:T(2,128)S(1)}, bf16[3,8,128,1024]{3,2,1,0:T(8,128)(2,1)S(1)}, bf16[3,8,512,128]{3,2,1,0:T(8,128)(2,1)S(1)}, s32[3,4,8]{2,1,0:T(4,128)S(1)}) custom-call(bf16[12,128,1024]{2,1,0:T(8,128)(2,1)} %bitcast.11, bf16[2,128,512]{2,1,0:T(8,128)(2,1)} %piece.1, s32[4,8]{1,0:T(4,128)} %bitcast.12, ...), custom_call_target="tpu_custom_call" | custom-call | tf_op jit(solution)/shard_map/exchange_of/pallas_call | solution.py:634
  86.0 6.4 %fock_of.1 = (f32[12,128,1024]{2,1,0:T(8,128)}, f32[2,128]{1,0:T(2,128)}) custom-call(s32[3,4,8]{2,1,0:T(4,128)S(1)} %get-tuple-element.9.names, bf16[3,8,512,128]{3,2,1,0:T(8,128)(2,1)S(1)} %get-tuple-element.10.basis_t, f32[24,128]{1,0:T(8,128)S(1)} %bitcast.10, bf16[3,8,128,1024]{3,2,1,0:T(8,128)(2,1)S(1)} %get-tuple-element.12.psi, ...), custom_call_target="tpu_custom_call" | custom-call | tf_op jit(solution)/shard_map/fock_of/pallas_call | solution.py:775

commit v7 on v6

--- a/solution.py
+++ b/solution.py
@@ -68,7 +68,7 @@
         info, info_buf, rows_out, rows_buf, scaled_out,
         load, list_sem, name_sent, name_got, v_sent, v_got, z_sent, chip_sent,
         part_sent, part_got, psi_sent, psi_got, passed, relay_sent, sent, got,
-        relay_v, v_passed, pair_sent, pair_got, v_first,
+        relay_v, v_passed, pair_sent, pair_got, v_first, word,
     ) = rest[12:]
     n_grid, n_atom = shape
     n = n_grid * n_atom
@@ -139,7 +139,49 @@
     ]
     for copy in loads:
         copy.start()
-    meet_all(shape)
+    early = n_atom <= 4
+
+    def greet_near():
+        barrier = pltpu.get_barrier_semaphore()
+
+        def greet(able, g, a):
+            @pl.when(able)
+            def _():
+                pl.semaphore_signal(barrier, inc=1, device_id=(g, a), device_id_type=MESH)
+
+        greet(grid >= 0, ig, atom)
+        greet(has_outer, og, atom)
+        greet(atom > 0, grid, atom - 1)
+        greet(atom < n_atom - 1, grid, atom + 1)
+        for g in (0, last):
+            greet(at_split, g, atom)
+        for g in (middle - 1, middle):
+            greet(relays, g, atom)
+        met = 1 + has_outer.astype(jnp.int32) + (atom > 0).astype(jnp.int32)
+        met = met + (atom < n_atom - 1).astype(jnp.int32)
+        met = met + 2 * jnp.logical_or(at_split, relays).astype(jnp.int32)
+        pl.semaphore_wait(barrier, met)
+
+    def pass_word(t):
+        for way, (step, when) in enumerate(((1, grid), (-1, last - grid))):
+            behind = grid > 0 if way == 0 else grid < last
+            ahead = grid < last if way == 0 else grid > 0
+            now = t == when * n_atom // n_grid
+
+            @pl.when(jnp.logical_and(now, behind))
+            def _():
+                pl.semaphore_wait(word.at[way], 1)
+
+            @pl.when(jnp.logical_and(now, ahead))
+            def _():
+                pl.semaphore_signal(
+                    word.at[way], inc=1, device_id=(grid + step, atom), device_id_type=MESH
+                )
+
+    if early:
+        greet_near()
+    else:
+        meet_all(shape)
 
     @pl.when(has_outer)
     def _():
@@ -197,7 +239,6 @@
         wrapped(start + run, total),
         mass,
     )
-    to_chips(info, info_buf, 1)
     info_buf[slot_here] = info[...]
 
     if relayed:
@@ -444,6 +485,9 @@
         @pl.when(t >= 1)
         def _():
             forward(0, t - 1)
+
+        if early:
+            pass_word(t)
 
         @pl.when(t >= 2)
         def _():
@@ -471,25 +515,12 @@
     for copy in loads[5:]:
         copy.wait()
     halves = scale.shape[1] // LANES
-    hand_over(info_buf, 1)
-    facts = info_buf[...].reshape(n * RUN, LANES)
-    same = (facts[:, 0:1] == mine).astype(jnp.float32)
-    mass = jnp.sum(same * facts[:, LANES // 2 : LANES // 2 + 1], axis=0, keepdims=True)
-    share = 1.0 / (1.0 + to_columns(mass)[:, 0:1])
-    same = same.reshape(n, RUN, LANES)
-    none = jnp.zeros_like(same)
-    selects = []
-    for h in range(halves):
-        full = jnp.concatenate(
-            [same if k == h else none for k in range(halves)], axis=1
-        ).reshape(n * RUN * halves, LANES)
-        selects.append(jnp.transpose(full).astype(jnp.bfloat16))
-
     forward(0, n_atom - 1)
     finish(n_atom - 1)
     dens_buf[atom] = dens[atom]
 
     wait_all(dens_buf, got.at[0], n_atom - 1)
+    to_chips(info, info_buf, 1)
     density = to_columns(2.0 * jnp.sum(dens_buf[...], axis=0))
     safe = jnp.where(density > 0.0, density, 1.0)
     radius = jnp.where(density > 0.0, jnp.exp(jnp.log(safe) * (1.0 / 3.0)), 0.0)[:, 0:1]
@@ -506,6 +537,21 @@
         to_chips(rows_out.at[layer], rows_buf.at[layer], 2 + layer)
         rows_buf[layer, slot_here] = rows_out[layer]
         send_psi(1 + layer)
+        if layer == 0:
+            hand_over(info_buf, 1)
+            facts = info_buf[...].reshape(n * RUN, LANES)
+            same = (facts[:, 0:1] == mine).astype(jnp.float32)
+            mass = jnp.sum(same * facts[:, LANES // 2 : LANES // 2 + 1], axis=0, keepdims=True)
+            share = 1.0 / (1.0 + to_columns(mass)[:, 0:1])
+            same = same.reshape(n, RUN, LANES)
+            none = jnp.zeros_like(same)
+            selects = []
+            for h in range(halves):
+                full = jnp.concatenate(
+                    [same if k == h else none for k in range(halves)], axis=1
+                ).reshape(n * RUN * halves, LANES)
+                selects.append(jnp.transpose(full).astype(jnp.bfloat16))
+
         hand_over(rows_buf.at[layer], 2 + layer)
         held = rows_buf[layer].reshape(n * RUN * halves, LANES)
         summed = jnp.concatenate(
@@ -681,6 +727,7 @@
             dma((2 + layers,)),
             dma((2 + layers,)),
             dma((nb,)),
+            pltpu.SemaphoreType.REGULAR((2,)),
         ],
         compiler_params=pltpu.CompilerParams(
             collective_id=0, has_side_effects=True, vmem_limit_bytes=grant

time: 92.6 us -> 92 us (level); the launches traced: 92.5 us -> 90.9 us
  Pallas kernels: 91.8 us -> 90.2 us
    pallas_call x1, Pallas kernels: 85.4 us -> 83.8 us  [exchange_of(): pl.pallas_call(functools.partial(exchange_kernel, shape, layers), out_sha...]
where the time goes in v7:
time: 92 us; the launch traced here: 90.9 us
  Pallas kernels  90.2 us (98%)
    pallas_call x1, Pallas kernels, exchange_of(): pl.pallas_call(functools.partial(exchange_kernel, shape, layers), out_sha...  83.8 us
    pallas_call x1, Pallas kernels, fock_of(): pl.pallas_call(fock_kernel, out_shape=(jax.ShapeDtypeStruct((owned, width...  6.41 us

profile of v7, /device:TPU:1, one launch (start us, length us, event | category | flops | bytes accessed | tf_op | source)
XLA Modules:
  0.0 90.9 jit_solution(922590318072790294)
XLA Ops:
  0.6 83.8 %exchange_of.1 = (f32[2,128]{1,0:T(2,128)S(1)}, f32[12,2,128]{2,1,0:T(2,128)S(1)}, bf16[3,8,128,1024]{3,2,1,0:T(8,128)(2,1)S(1)}, bf16[3,8,512,128]{3,2,1,0:T(8,128)(2,1)S(1)}, s32[3,4,8]{2,1,0:T(4,128)S(1)}) custom-call(bf16[12,128,1024]{2,1,0:T(8,128)(2,1)} %bitcast.11, bf16[2,128,512]{2,1,0:T(8,128)(2,1)} %piece.1, s32[4,8]{1,0:T(4,128)} %bitcast.12, ...), custom_call_target="tpu_custom_call" | custom-call | tf_op jit(solution)/shard_map/exchange_of/pallas_call | solution.py:680
  84.5 6.4 %fock_of.1 = (f32[12,128,1024]{2,1,0:T(8,128)}, f32[2,128]{1,0:T(2,128)}) custom-call(s32[3,4,8]{2,1,0:T(4,128)S(1)} %get-tuple-element.9.names, bf16[3,8,512,128]{3,2,1,0:T(8,128)(2,1)S(1)} %get-tuple-element.10.basis_t, f32[24,128]{1,0:T(8,128)S(1)} %bitcast.10, bf16[3,8,128,1024]{3,2,1,0:T(8,128)(2,1)S(1)} %get-tuple-element.12.psi, ...), custom_call_target="tpu_custom_call" | custom-call | tf_op jit(solution)/shard_map/fock_of/pallas_call | solution.py:822

commit v8 on v7

--- a/solution.py
+++ b/solution.py
@@ -234,11 +234,9 @@
     for i in range(nb):
         here = jnp.where(place[i : i + 1, :] == run, weights[i : i + 1, :], 0.0)
         mass = mass + jnp.sum(here, axis=1, keepdims=True)
-    info[...] = jnp.where(
-        lax.broadcasted_iota(jnp.int32, (RUN, LANES), 1) < LANES // 2,
-        wrapped(start + run, total),
-        mass,
-    )
+    own_lane = lax.broadcasted_iota(jnp.int32, (RUN, LANES), 1).astype(jnp.float32)
+    masses = jnp.sum(jnp.where(own_lane == run + LANES // 2, mass, 0.0), axis=0, keepdims=True)
+    info[...] = jnp.where(lane < LANES // 2, mine, masses)
     info_buf[slot_here] = info[...]
 
     if relayed:
@@ -539,9 +537,14 @@
         send_psi(1 + layer)
         if layer == 0:
             hand_over(info_buf, 1)
-            facts = info_buf[...].reshape(n * RUN, LANES)
-            same = (facts[:, 0:1] == mine).astype(jnp.float32)
-            mass = jnp.sum(same * facts[:, LANES // 2 : LANES // 2 + 1], axis=0, keepdims=True)
+            facts = jnp.broadcast_to(info_buf[...], (n, RUN, LANES)).reshape(n * RUN, LANES)
+            row = lax.rem(lax.broadcasted_iota(jnp.int32, (n * RUN, LANES), 0), RUN)
+            lanes = lax.broadcasted_iota(jnp.int32, (n * RUN, LANES), 1)
+            named = jnp.sum(jnp.where(lanes == row, facts, 0.0), axis=1, keepdims=True)
+            held_mass = jnp.where(lanes == row + LANES // 2, facts, 0.0)
+            same = (named == mine).astype(jnp.float32)
+            held_mass = jnp.sum(held_mass, axis=1, keepdims=True)
+            mass = jnp.sum(same * held_mass, axis=0, keepdims=True)
             share = 1.0 / (1.0 + to_columns(mass)[:, 0:1])
             same = same.reshape(n, RUN, LANES)
             none = jnp.zeros_like(same)
@@ -701,8 +704,8 @@
             pltpu.VMEM((2, n_atom, nb // 2, points, columns), bf16),
             pltpu.VMEM((n_atom, nb, points), f32),
             pltpu.VMEM((n_atom, nb, points), f32),
-            pltpu.VMEM((RUN, LANES), f32),
-            pltpu.VMEM((n, RUN, LANES), f32),
+            pltpu.VMEM((1, LANES), f32),
+            pltpu.VMEM((n, 1, LANES), f32),
             pltpu.VMEM((layers, packed, LANES), bf16),
             pltpu.VMEM((layers, n, packed, LANES), bf16),
             pltpu.VMEM((nb, points), f32),

time: 92 us -> 91.6 us (level)
  no operation moved by 1% of the time
where the time goes in v8:
time: 91.6 us; the launch traced here: 90.2 us
  Pallas kernels  89.6 us (98%)
    pallas_call x1, Pallas kernels, exchange_of(): pl.pallas_call(functools.partial(exchange_kernel, shape, layers), out_sha...  83.2 us
    pallas_call x1, Pallas kernels, fock_of(): pl.pallas_call(fock_kernel, out_shape=(jax.ShapeDtypeStruct((owned, width...  6.37 us

profile of v8, /device:TPU:1, one launch (start us, length us, event | category | flops | bytes accessed | tf_op | source)
XLA Modules:
  0.0 90.2 jit_solution(8032427294095881622)
XLA Ops:
  0.6 83.2 %exchange_of.1 = (f32[2,128]{1,0:T(2,128)S(1)}, f32[12,2,128]{2,1,0:T(2,128)S(1)}, bf16[3,8,128,1024]{3,2,1,0:T(8,128)(2,1)S(1)}, bf16[3,8,512,128]{3,2,1,0:T(8,128)(2,1)S(1)}, s32[3,4,8]{2,1,0:T(4,128)S(1)}) custom-call(bf16[12,128,1024]{2,1,0:T(8,128)(2,1)} %bitcast.11, bf16[2,128,512]{2,1,0:T(8,128)(2,1)} %piece.1, s32[4,8]{1,0:T(4,128)} %bitcast.12, ...), custom_call_target="tpu_custom_call" | custom-call | tf_op jit(solution)/shard_map/exchange_of/pallas_call | solution.py:683
  83.8 6.4 %fock_of.1 = (f32[12,128,1024]{2,1,0:T(8,128)}, f32[2,128]{1,0:T(2,128)}) custom-call(s32[3,4,8]{2,1,0:T(4,128)S(1)} %get-tuple-element.9.names, bf16[3,8,512,128]{3,2,1,0:T(8,128)(2,1)S(1)} %get-tuple-element.10.basis_t, f32[24,128]{1,0:T(8,128)S(1)} %bitcast.10, bf16[3,8,128,1024]{3,2,1,0:T(8,128)(2,1)S(1)} %get-tuple-element.12.psi, ...), custom_call_target="tpu_custom_call" | custom-call | tf_op jit(solution)/shard_map/fock_of/pallas_call | solution.py:825

commit v9 on v8

--- a/solution.py
+++ b/solution.py
@@ -606,6 +606,8 @@
         wait_all(near, got.at[final + 2 - side], n_atom)
 
     wait_all(near, got.at[final + 1 + side], n_atom)
+
+    all_names[...] = jnp.minimum(jnp.maximum(all_names[...] - first + 1, 0), owned + 1)
 
     @pl.loop(0, n_atom)
     def _(q):
@@ -753,7 +755,6 @@
     picks = depth // width
     most = groups * count * picks
     tile = min(columns, TILE)
-    first = lax.axis_index("grid") * owned
     last = pltpu.make_async_copy(pot, pot_out, done.at[owned])
     last.start()
 
@@ -766,7 +767,7 @@
         @pl.loop(0, count)
         def _(b):
             for j in range(picks):
-                row = jnp.minimum(jnp.maximum(names[k, j, b] - first + 1, 0), owned + 1)
+                row = names[k, j, b]
                 n = filled[row]
                 table[row * most + n] = (k * count + b) * picks + j
                 filled[row] = n + 1

time: 91.6 us -> 91 us (level)
  no operation moved by 1% of the time
where the time goes in v9:
time: 91 us; the launch traced here: 90.2 us
  Pallas kernels  89.6 us (98%)
    pallas_call x1, Pallas kernels, exchange_of(): pl.pallas_call(functools.partial(exchange_kernel, shape, layers), out_sha...  83.2 us
    pallas_call x1, Pallas kernels, fock_of(): pl.pallas_call(fock_kernel, out_shape=(jax.ShapeDtypeStruct((owned, width...  6.38 us

profile of v9, /device:TPU:1, one launch (start us, length us, event | category | flops | bytes accessed | tf_op | source)
XLA Modules:
  0.0 90.2 jit_solution(17634970702432976577)
XLA Ops:
  0.6 83.2 %exchange_of.1 = (f32[2,128]{1,0:T(2,128)S(1)}, f32[12,2,128]{2,1,0:T(2,128)S(1)}, bf16[3,8,128,1024]{3,2,1,0:T(8,128)(2,1)S(1)}, bf16[3,8,512,128]{3,2,1,0:T(8,128)(2,1)S(1)}, s32[3,4,8]{2,1,0:T(4,128)S(1)}) custom-call(bf16[12,128,1024]{2,1,0:T(8,128)(2,1)} %bitcast.11, bf16[2,128,512]{2,1,0:T(8,128)(2,1)} %piece.1, s32[4,8]{1,0:T(4,128)} %bitcast.12, ...), custom_call_target="tpu_custom_call" | custom-call | tf_op jit(solution)/shard_map/exchange_of/pallas_call | solution.py:685
  83.8 6.4 %fock_of.1 = (f32[12,128,1024]{2,1,0:T(8,128)}, f32[2,128]{1,0:T(2,128)}) custom-call(s32[3,4,8]{2,1,0:T(4,128)S(1)} %get-tuple-element.9.names, bf16[3,8,512,128]{3,2,1,0:T(8,128)(2,1)S(1)} %get-tuple-element.10.basis_t, f32[24,128]{1,0:T(8,128)S(1)} %bitcast.10, bf16[3,8,128,1024]{3,2,1,0:T(8,128)(2,1)S(1)} %get-tuple-element.12.psi, ...), custom_call_target="tpu_custom_call" | custom-call | tf_op jit(solution)/shard_map/fock_of/pallas_call | solution.py:826
